TPU v7x, 512 devices: a whole 4x8x8 slice. The times are simulated.
512 devices in a mesh: users: 32 (over x, z_hi, core), hist: 16 (over y, z_lo).
Axes of the slice: x: 4, y: 8, z: 8 (z_hi: 4, z_lo: 2; z = z_hi * 2 + z_lo), core: 2. Of those that a mesh axis runs over, the one named last changes fastest.
Arguments:
- cand_x: bfloat16 [32768, 512], P(('users', 'hist')), parts along dimension 0, may hold values from -6 to 6
- hist_keys: bfloat16 [262144, 512], P(('users', 'hist')), parts along dimension 0, may hold values from -6 to 6
- hist_values: bfloat16 [262144, 512], P(('users', 'hist')), parts along dimension 0, may hold values from -6 to 6
- key_scale: bfloat16 [262144], P(('users', 'hist')), parts along dimension 0, may hold values from 0.5 to 2
- hist_len: int32 [32], P('users'), parts along dimension 0, may hold values from 2048 to 8192
- cand_limit: int32 [32768], P('users'), parts along dimension 0, may hold values from 1 to 8192
- ln_gain: float32 [512], replicated, may hold values from 0.1 to 1.9
- w_qu: bfloat16 [512, 1024], replicated, may hold values from -0.25 to 0.25
- w_out: bfloat16 [512, 512], replicated, may hold values from -0.25 to 0.25
Outputs:
- scored: bfloat16 [32768, 512], P(('users', 'hist')), parts along dimension 0
There are 32 independent parts, one for each index of `users`. A program takes and returns all parts, laid end to end along the dimension named above; an argument that names none is the same for every part. Nothing has to cross between parts.
All inputs are finite; a program needn't handle non-finite values.
Results may differ from a plain program's by a relative error of at most 0.0058.
Values may be sent and summed in bfloat16 or wider, within the bound.
No kernel may reach another device: no remote copies, remote signals or barrier semaphores. Data moves between devices by JAX's collectives and lax.ppermute only.
A program may use at most 64 MiB of HBM per device.

v0:
```python
import jax
import jax.numpy as jnp
from jax import lax
from jax.sharding import PartitionSpec as P

HEADS = 8


def in_order(tiles, dim):
    shape = list(tiles.shape[1:])
    shape[dim] *= tiles.shape[0]
    return jnp.moveaxis(tiles, 0, dim).reshape(shape)


def from_everyone(value, axis):
    copies = jnp.broadcast_to(value, (lax.axis_size(axis), *value.shape))
    return lax.all_to_all(copies, axis, split_axis=0, concat_axis=0, tiled=True)


def gather_directly(value, axis, dim):
    return in_order(from_everyone(value, axis), dim)


def in_blocks(value, dim, peers):
    before, after = (value.shape[:dim], value.shape[dim + 1 :])
    return jnp.moveaxis(value.reshape(*before, peers, -1, *after), dim, 0)


def sum_at_owner(value, axis, dim):
    peers = lax.axis_size(axis)
    tiles = lax.all_to_all(in_blocks(value, dim, peers), axis, 0, 0, tiled=True)
    return jnp.sum(tiles.astype(jnp.float32), axis=0)


def row_norm(values):
    center = jnp.mean(values, axis=-1, keepdims=True)
    spread = jnp.mean((values - center) ** 2, axis=-1, keepdims=True)
    return (values - center) / jnp.sqrt(spread + 1e-05)


def attend(query_rows, history_limits, key_rows, value_rows, scale_rows, offset_pos):
    count = query_rows.shape[0]
    length = key_rows.shape[0]
    width = query_rows.shape[1]
    head_size = width // HEADS
    query_head_blocks = query_rows.reshape(count, HEADS, head_size)
    key_head_blocks = key_rows.reshape(length, HEADS, head_size)
    value_head_blocks = value_rows.reshape(length, HEADS, head_size)
    attention_scores = jnp.einsum(
        "ufe,yfe->fuy", query_head_blocks, key_head_blocks, preferred_element_type=jnp.float32
    )
    factor = scale_rows.astype(jnp.float32) / jnp.sqrt(jnp.float32(head_size))
    attention_scores = attention_scores * factor[None, None, :]
    positions = offset_pos + jnp.arange(length, dtype=jnp.int32)
    visible = positions[None, :] < history_limits[:, None]
    weight_matrices = jnp.where(visible[None], jax.nn.silu(attention_scores), 0.0).astype(
        jnp.bfloat16
    )
    summed_output = jnp.einsum(
        "apn,naf->paf", weight_matrices, value_head_blocks, preferred_element_type=jnp.float32
    )
    return summed_output.reshape(count, width)


def on_device(
    cand_x, hist_keys, hist_values, key_scale, hist_len, cand_limit, ln_gain, w_qu, w_out
):
    own_rows = cand_x.shape[0]
    width = cand_x.shape[1]
    inputs32 = cand_x.astype(jnp.float32)
    normed = (row_norm(inputs32) * ln_gain).astype(jnp.bfloat16)
    projected = jax.nn.silu(jnp.dot(normed, w_qu, preferred_element_type=jnp.float32))
    query_vectors = projected[:, :width].astype(jnp.bfloat16)
    gating = projected[:, width:]
    all_limits = jnp.minimum(cand_limit, hist_len[0])
    my_index = lax.axis_index("hist")
    offset_pos = my_index * hist_keys.shape[0]
    every_query = gather_directly(query_vectors, "hist", 0)
    block_rows = own_rows * lax.axis_size("hist")
    while block_rows > 256 and block_rows % 2 == 0:
        block_rows = block_rows // 2
    blocks = own_rows * lax.axis_size("hist") // block_rows

    def one_block(couple):
        return attend(couple[0], couple[1], hist_keys, hist_values, key_scale, offset_pos)

    outputs = lax.map(
        one_block,
        (every_query.reshape(blocks, block_rows, width), all_limits.reshape(blocks, block_rows)),
    )
    attended = sum_at_owner(
        outputs.reshape(own_rows * lax.axis_size("hist"), width).astype(jnp.bfloat16), "hist", 0
    )
    mixed = (row_norm(attended) * gating).astype(jnp.bfloat16)
    return (inputs32 + jnp.dot(mixed, w_out, preferred_element_type=jnp.float32)).astype(
        jnp.bfloat16
    )


def solution(mesh):
    in_specs = (
        P(("users", "hist"), None),
        P(("users", "hist"), None),
        P(("users", "hist"), None),
        P(("users", "hist")),
        P("users"),
        P("users"),
        P(),
        P(),
        P(),
    )
    out_specs = P(("users", "hist"), None)
    return jax.shard_map(
        on_device, mesh=mesh, in_specs=in_specs, out_specs=out_specs, check_vma=False
    )
```

profile of v0, /device:TPU:6, one launch (start us, length us, event | category | flops | bytes accessed | tf_op | source)
XLA Modules:
  0.0 95.0 jit_solution(10306071548147074511)
XLA Ops:
  0.0 0.0 copy-start
  0.0 1.0 %convert_reduce_fusion.2 = f32[64]{0:T(128)S(1)} fusion(bf16[64,512]{1,0:T(8,128)(2,1)} %param.11), kind=kLoop, calls=%fused_computation.16 | loop fusion | flops 65472 | bytes 65792 | tf_op jit(solution)/shard_map/reduce_sum | solution.py:36
  1.1 1.0 %fusion.6 = f32[64]{0:T(128)S(1)} fusion(bf16[64,512]{1,0:T(8,128)(2,1)} %param.11, f32[64]{0:T(128)S(1)} %broadcast_multiply_fusion.1), kind=kLoop, calls=%fused_computation.19 | loop fusion | flops 131008 | bytes 66048 | tf_op jit(solution)/shard_map/reduce_sum | solution.py:37
  2.1 0.0 copy-done
  2.1 1.2 %divide_multiply_fusion = f32[64,1024]{1,0:T(8,128)S(1)} fusion(bf16[512,1024]{1,0:T(8,128)(2,1)S(1)} %copy-done, bf16[64,512]{1,0:T(8,128)(2,1)} %param.11, f32[512]{0:T(512)} %param.17, f32[64]{0:T(128)S(1)} %add_sqrt_fusion.1, f32[64]{0:T(128)S(1)} %broadcast_multiply_fusion.1), kind=kOutput, calls=%fused_computation.14 | convolution fusion | flops 67534848 | bytes 1378816 | tf_op jit(solution)/shard_map/dot_general | solution.py:72
  3.4 1.1 %broadcast_in_dim.32 = bf16[16,64,512]{2,1,0:T(8,128)(2,1)} broadcast(bf16[64,512]{1,0:T(8,128)(2,1)S(1)} %slice.16), dimensions={1,2} | broadcast | bytes 1114112 | tf_op jit(solution)/shard_map/broadcast_in_dim | solution.py:16
  4.5 9.1 %all-to-all-start = ((bf16[16,64,512]{2,1,0:T(8,128)(2,1)}), bf16[16,64,512]{2,1,0:T(8,128)(2,1)S(1)}, u32[]{:S(2)}, u32[]{:S(2)}) async-start(bf16[16,64,512]{2,1,0:T(8,128)(2,1)} %broadcast_in_dim.32), calls=%async_computation | async-start | bytes 2097152 | tf_op jit(solution)/shard_map/all_to_all | solution.py:17
  13.6 0.0 copy-start.2
  13.7 0.0 copy-done.1
  13.7 0.0 copy-start.6
  13.7 0.0 copy-start.5
  13.7 1.0 %copy.13 = bf16[512,512]{0,1:T(8,128)(2,1)} copy(bf16[512,512]{1,0:T(8,128)(2,1)S(1)} %copy-done.1) | data formatting | bytes 1048576 | tf_op jit(solution)/shard_map/while | solution.py:87
  14.7 0.0 copy-done.2
  14.7 1.0 %copy.14 = bf16[512,512]{0,1:T(8,128)(2,1)} copy(bf16[512,512]{1,0:T(8,128)(2,1)S(1)} %copy-done.2) | data formatting | bytes 1048576 | tf_op jit(solution)/shard_map/while | solution.py:87
  16.4 0.0 copy-done.6
  16.4 25.9 %all-to-all-done = bf16[16,64,512]{2,1,0:T(8,128)(2,1)S(1)} async-done(((bf16[16,64,512]{2,1,0:T(8,128)(2,1)}), bf16[16,64,512]{2,1,0:T(8,128)(2,1)S(1)}, u32[]{:S(2)}, u32[]{:S(2)}) %all-to-all-start) | async-done | bytes 1048608 | tf_op jit(solution)/shard_map/all_to_all | solution.py:17
  42.4 0.0 copy-done.5
  42.4 19.2 %while.10 = (s32[]{:T(128)}, bf16[4,256,512]{2,1,0:T(8,128)(2,1)}, s32[]{:T(128)}, s32[4,256]{1,0:T(4,128)S(1)}, bf16[4,256,512]{2,1,0:T(8,128)(2,1)S(1)}, /*ind...) while((s32[]{:T(128)}, bf16[4,256,512]{2,1,0:T(8,128)(2,1)}, ...), condition=%wide.region_3.4_spmd, body=%wide.region_2.3_spmd.sunk | while | flops 275908096 | bytes 6042245 | solution.py:87
  42.4 0.1 broadcast_compare_fusion.2
  42.6 0.1 copy.26
  42.7 0.7 copy-done.3
  43.4 2.9 %fusion.32 = bf16[8,256,64]{1,2,0:T(8,128)(2,1)S(1)} fusion(bf16[512,8,64]{0,2,1:T(8,128)(2,1)} %bitcast.37, bf16[256,8,64]{0,2,1:T(8,128)(2,1)S(1)} %bitcast.32, bf16[512,8,64]{0,2,1:T(8,128)(2,1)S(1)} %bitcast.36, f32[512]{0:T(512)S(1)} %convert_multiply_fusion.2, pred[256,512]{1,0:T(8,128)(4,1)S(1)} %broadcast_compare_fusion.2), kind=kOutput, calls=%fused_computation.1.clone.1 | convolution fusion | flops 275775488 | bytes 1705984 | tf_op jit(solution)/shard_map/while/body/eval_jaxpr/apn,naf->paf/dot_general | solution.py:59
  46.3 0.1 copy.27
  46.5 0.7 constant_dynamic-update-slice_fusion.2
  47.2 0.1 broadcast_compare_fusion.2
  47.4 0.1 copy.26
  47.5 0.7 copy-done.3
  48.2 2.9 %fusion.32 = bf16[8,256,64]{1,2,0:T(8,128)(2,1)S(1)} fusion(bf16[512,8,64]{0,2,1:T(8,128)(2,1)} %bitcast.37, bf16[256,8,64]{0,2,1:T(8,128)(2,1)S(1)} %bitcast.32, bf16[512,8,64]{0,2,1:T(8,128)(2,1)S(1)} %bitcast.36, f32[512]{0:T(512)S(1)} %convert_multiply_fusion.2, pred[256,512]{1,0:T(8,128)(4,1)S(1)} %broadcast_compare_fusion.2), kind=kOutput, calls=%fused_computation.1.clone.1 | convolution fusion | flops 275775488 | bytes 1705984 | tf_op jit(solution)/shard_map/while/body/eval_jaxpr/apn,naf->paf/dot_general | solution.py:59
  51.1 0.1 copy.27
  51.3 0.7 constant_dynamic-update-slice_fusion.2
  52.0 0.1 broadcast_compare_fusion.2
  52.2 0.1 copy.26
  52.3 0.7 copy-done.3
  53.0 2.9 %fusion.32 = bf16[8,256,64]{1,2,0:T(8,128)(2,1)S(1)} fusion(bf16[512,8,64]{0,2,1:T(8,128)(2,1)} %bitcast.37, bf16[256,8,64]{0,2,1:T(8,128)(2,1)S(1)} %bitcast.32, bf16[512,8,64]{0,2,1:T(8,128)(2,1)S(1)} %bitcast.36, f32[512]{0:T(512)S(1)} %convert_multiply_fusion.2, pred[256,512]{1,0:T(8,128)(4,1)S(1)} %broadcast_compare_fusion.2), kind=kOutput, calls=%fused_computation.1.clone.1 | convolution fusion | flops 275775488 | bytes 1705984 | tf_op jit(solution)/shard_map/while/body/eval_jaxpr/apn,naf->paf/dot_general | solution.py:59
  55.9 0.1 copy.27
  56.1 0.7 constant_dynamic-update-slice_fusion.2
  56.8 0.1 broadcast_compare_fusion.2
  57.0 0.1 copy.26
  57.1 0.7 copy-done.3
  57.8 2.9 %fusion.32 = bf16[8,256,64]{1,2,0:T(8,128)(2,1)S(1)} fusion(bf16[512,8,64]{0,2,1:T(8,128)(2,1)} %bitcast.37, bf16[256,8,64]{0,2,1:T(8,128)(2,1)S(1)} %bitcast.32, bf16[512,8,64]{0,2,1:T(8,128)(2,1)S(1)} %bitcast.36, f32[512]{0:T(512)S(1)} %convert_multiply_fusion.2, pred[256,512]{1,0:T(8,128)(4,1)S(1)} %broadcast_compare_fusion.2), kind=kOutput, calls=%fused_computation.1.clone.1 | convolution fusion | flops 275775488 | bytes 1705984 | tf_op jit(solution)/shard_map/while/body/eval_jaxpr/apn,naf->paf/dot_general | solution.py:59
  60.7 0.1 copy.27
  60.9 0.7 constant_dynamic-update-slice_fusion.2
  61.6 31.4 %all_to_all.10 = bf16[16,64,512]{2,1,0:T(8,128)(2,1)S(1)} all-to-all(bf16[16,64,512]{2,1,0:T(8,128)(2,1)} %bitcast.35), channel_id=1, replica_groups=mesh['users'=32,'hist'=16] {'hist'}, dimensions={0} | all-to-all | bytes 2097152 | tf_op jit(solution)/shard_map/all_to_all | solution.py:31
  93.0 0.3 convert_reduce_fusion
  93.3 0.2 multiply_reduce_fusion
  93.5 0.3 copy-done.4
  93.9 0.2 copy-done.7
  94.1 0.9 fusion.3
  (31 shorter events, 0.2 us)
Async XLA Ops:
  0.0 2.1 %copy-start = (bf16[512,1024]{1,0:T(8,128)(2,1)S(1)}, bf16[512,1024]{1,0:T(8,128)(2,1)}, u32[]{:S(2)}) copy-start(bf16[512,1024]{1,0:T(8,128)(2,1)} %param.18) | copy-start | bytes 3145732
  4.5 9.2 %copy-start.1 = (bf16[512,512]{1,0:T(8,128)(2,1)S(1)}, bf16[512,512]{1,0:T(8,128)(2,1)}, u32[]{:S(2)}) copy-start(bf16[512,512]{1,0:T(8,128)(2,1)} %param.12) | copy-start | bytes 1572868
  4.5 37.9 %all-to-all-start = ((bf16[16,64,512]{2,1,0:T(8,128)(2,1)}), bf16[16,64,512]{2,1,0:T(8,128)(2,1)S(1)}, u32[]{:S(2)}, u32[]{:S(2)}) async-start(bf16[16,64,512]{2,1,0:T(8,128)(2,1)} %broadcast_in_dim.32), calls=%async_computation | async-start | bytes 2097152 | tf_op jit(solution)/shard_map/all_to_all | solution.py:17
  13.6 1.1 %copy-start.2 = (bf16[512,512]{1,0:T(8,128)(2,1)S(1)}, bf16[512,512]{1,0:T(8,128)(2,1)}, u32[]{:S(2)}) copy-start(bf16[512,512]{1,0:T(8,128)(2,1)} %param.13) | copy-start | bytes 1572868
  13.7 2.7 %copy-start.6 = (s32[1024]{0:T(1024)S(1)}, s32[1024]{0:T(1024)}, u32[]{:S(2)}) copy-start(s32[1024]{0:T(1024)} %param.16) | copy-start | bytes 12292
  13.7 28.7 %copy-start.5 = (bf16[512]{0:T(512)(128)(2,1)S(1)}, bf16[512]{0:T(512)(128)(2,1)}, u32[]{:S(2)}) copy-start(bf16[512]{0:T(512)(128)(2,1)} %param.14) | copy-start | bytes 3076
  42.4 1.0 %copy-start.3 = (bf16[512,512]{0,1:T(8,128)(2,1)S(1)}, bf16[512,512]{0,1:T(8,128)(2,1)}, u32[]{:S(2)}) copy-start(bf16[512,512]{0,1:T(8,128)(2,1)} %get-tuple-element.154) | copy-start | bytes 1572868 | tf_op jit(solution)/shard_map/while
  47.2 1.0 %copy-start.3 = (bf16[512,512]{0,1:T(8,128)(2,1)S(1)}, bf16[512,512]{0,1:T(8,128)(2,1)}, u32[]{:S(2)}) copy-start(bf16[512,512]{0,1:T(8,128)(2,1)} %get-tuple-element.154) | copy-start | bytes 1572868 | tf_op jit(solution)/shard_map/while
  52.0 1.0 %copy-start.3 = (bf16[512,512]{0,1:T(8,128)(2,1)S(1)}, bf16[512,512]{0,1:T(8,128)(2,1)}, u32[]{:S(2)}) copy-start(bf16[512,512]{0,1:T(8,128)(2,1)} %get-tuple-element.154) | copy-start | bytes 1572868 | tf_op jit(solution)/shard_map/while
  56.8 1.0 %copy-start.3 = (bf16[512,512]{0,1:T(8,128)(2,1)S(1)}, bf16[512,512]{0,1:T(8,128)(2,1)}, u32[]{:S(2)}) copy-start(bf16[512,512]{0,1:T(8,128)(2,1)} %get-tuple-element.154) | copy-start | bytes 1572868 | tf_op jit(solution)/shard_map/while
  93.0 0.8 copy-start.4
  93.0 1.1 %copy-start.7 = (bf16[512,512]{1,0:T(8,128)(2,1)S(1)}, bf16[512,512]{1,0:T(8,128)(2,1)}, u32[]{:S(2)}) copy-start(bf16[512,512]{1,0:T(8,128)(2,1)} %param.19) | copy-start | bytes 1572868
where the time goes:
time: 95.8 us; the launch traced here: 95 us
  blocking collectives  31.4 us (33%)
  waiting for transfers between devices  25.9 us (27%)
  matrix products  13.7 us (14%)
  local copies, waits for them, and re-layouts  10.7 us (11%)
  starting transfers between devices  9.15 us (10%)
  other arithmetic  3.16 us (3%)
    all_to_all x1, blocking collectives, sum_at_owner(): tiles = lax.all_to_all(in_blocks(value, dim, peers), axis, 0, 0, tiled=True)  31.4 us
    all_to_all x1, waiting for transfers between devices, from_everyone(): return lax.all_to_all(copies, axis, split_axis=0, concat_axis=0, tiled=True)  25.9 us
    dot_general x4, matrix products, attend(): jnp.einsum('apn,naf->paf', weight_matrices, value_head_blocks, preferred_...  11.5 us
    all_to_all x1, starting transfers between devices, from_everyone(): return lax.all_to_all(copies, axis, split_axis=0, concat_axis=0, tiled=True)  9.15 us
    dynamic_update_slice x8, local copies, waits for them, and re-layouts, on_device(): lax.map(one_block, (every_query.reshape(blocks, block_rows, width), all_l...  3.48 us
    while x8, local copies, waits for them, and re-layouts  2.78 us
    while x2, local copies, waits for them, and re-layouts, on_device(): lax.map(one_block, (every_query.reshape(blocks, block_rows, width), all_l...  2.03 us
  transfers between devices with their start and end apart: 1, of which 1 were waited for; matrix products, arithmetic and copies ran while one was open for 2% of the time, Pallas kernels for 0%

commit v1 on v0

v1 whole, which is shorter than its diff:
```python
import jax
import jax.numpy as jnp
from jax import lax
from jax.experimental import pallas as pl
from jax.experimental.pallas import tpu as pltpu
from jax.sharding import Mesh, PartitionSpec as P


F32 = jnp.float32
BF16 = jnp.bfloat16
VM = pl.BlockSpec(memory_space=pltpu.VMEM)
SM = pl.BlockSpec(memory_space=pltpu.SMEM)
PARAMS = pltpu.CompilerParams(vmem_limit_bytes=40 * 1024 * 1024)


def center(v):
    mean = jnp.mean(v, axis=-1, keepdims=True)
    var = jnp.mean((v - mean) ** 2, axis=-1, keepdims=True)
    return (v - mean) / jnp.sqrt(var + 1e-5)


def project_kernel(x_ref, gain_ref, w_ref, q_ref, gate_ref):
    normed = (center(x_ref[...].astype(F32)) * gain_ref[...]).astype(BF16)
    p = jnp.dot(normed, w_ref[...], preferred_element_type=F32)
    p = p / (1.0 + jnp.exp(-p))
    width = p.shape[1] // 2
    q = p[:, :width].astype(BF16)
    for i in range(q_ref.shape[0]):
        q_ref[i] = q
    gate_ref[...] = p[:, width:]


def scale_kernel(k_ref, s_ref, o_ref):
    rows = k_ref.shape[0]
    col = jnp.broadcast_to(s_ref[...].astype(F32) * (1.0 / 16.0), (8, rows)).T[:, :1]
    o_ref[...] = (k_ref[...].astype(F32) * col).astype(BF16)


def attend_kernel(off_ref, q_ref, k0_ref, v0_ref, k1_ref, v1_ref, lim_ref, o_ref):
    rows = q_ref.shape[0]
    n = k0_ref.shape[0]
    R = 256
    lane = lax.broadcasted_iota(jnp.int32, (1, 128), 1)
    low = lane < 64
    for r in range(rows // R):
        rs = slice(r * R, (r + 1) * R)
        masks = []
        for s in range(2):
            pos = lax.broadcasted_iota(jnp.int32, (R, n), 1) + off_ref[s]
            masks.append(jnp.where(pos < lim_ref[rs], 1.0, 0.0).astype(BF16))
        for pair in range(q_ref.shape[1] // 128):
            cs = slice(pair * 128, (pair + 1) * 128)
            q = q_ref[rs, cs]
            acc = jnp.zeros((R, 128), F32)
            for s, (kr, vr) in enumerate(((k0_ref, v0_ref), (k1_ref, v1_ref))):
                k = kr[:, cs]
                v = vr[:, cs]
                for sel in (low, jnp.logical_not(low)):
                    qh = jnp.where(sel, q, jnp.zeros_like(q))
                    vh = jnp.where(sel, v, jnp.zeros_like(v))
                    u = lax.dot_general(qh, k, (((1,), (1,)), ((), ())), preferred_element_type=F32)
                    w = (u * (1.0 + jnp.tanh(u))).astype(BF16) * masks[s]
                    acc += jnp.dot(w, vh, preferred_element_type=F32)
            o_ref[rs, cs] = acc.astype(BF16)


def finish_kernel(t_ref, gate_ref, x_ref, w_ref, o_ref):
    total = jnp.sum(t_ref[...].astype(F32), axis=0)
    mixed = (center(total) * gate_ref[...]).astype(BF16)
    o_ref[...] = (x_ref[...].astype(F32) + jnp.dot(mixed, w_ref[...], preferred_element_type=F32)).astype(BF16)


def sds(shape, dtype=BF16):
    return jax.ShapeDtypeStruct(shape, dtype)


def layer(cand_x, hist_keys, hist_values, key_scale, hist_len, cand_limit, ln_gain, w_qu, w_out):
    own, width = cand_x.shape
    n = hist_keys.shape[0]
    ny = lax.axis_size("y")
    nz = lax.axis_size("z")
    y = lax.axis_index("y")
    z = lax.axis_index("z")
    swap = [(i, 1 - i) for i in range(nz)]

    def exchange(t):
        return lax.all_to_all(t.reshape(ny, own, width), "y", 0, 0, tiled=True)

    def swapped(t):
        return lax.ppermute(t, "z", swap)

    v_far = swapped(hist_values)
    q, gate = pl.pallas_call(
        project_kernel,
        out_shape=(sds((ny, own, width)), sds((own, width), F32)),
        in_specs=[VM] * 3, out_specs=(VM,) * 2, compiler_params=PARAMS, name="project",
    )(cand_x, ln_gain.reshape(1, width), w_qu)
    every_q = exchange(q).reshape(ny * own, width)
    k_own = pl.pallas_call(
        scale_kernel, out_shape=sds((n, width)), in_specs=[VM] * 2, out_specs=VM,
        compiler_params=PARAMS, name="scale",
    )(hist_keys, key_scale.reshape(1, n))
    k_far = swapped(k_own)

    limits = jnp.minimum(cand_limit, hist_len[0]).reshape(ny, nz, own)
    limits = lax.dynamic_index_in_dim(limits, z, 1, keepdims=False).reshape(ny * own, 1)
    offsets = jnp.stack([(y * nz + z) * n, (y * nz + 1 - z) * n]).astype(jnp.int32)

    outs = pl.pallas_call(
        attend_kernel, out_shape=sds((ny * own, width)), in_specs=[SM] + [VM] * 6, out_specs=VM,
        compiler_params=PARAMS, name="attend",
    )(offsets, every_q, k_own, hist_values, k_far, v_far, limits)
    totals = exchange(outs)
    return pl.pallas_call(
        finish_kernel, out_shape=sds((own, width)), in_specs=[VM] * 4, out_specs=VM,
        compiler_params=PARAMS, name="finish",
    )(totals, gate, cand_x, w_out)


def solution(mesh):
    users, hist = mesh.devices.shape
    grid = Mesh(mesh.devices.reshape(users, hist // 2, 2), ("users", "y", "z"))
    both = ("users", "y", "z")
    in_specs = (P(both, None), P(both, None), P(both, None), P(both), P("users"), P("users"), P(), P(), P())
    return jax.shard_map(
        layer, mesh=grid, in_specs=in_specs, out_specs=P(both, None), check_vma=False
    )
```

time: 95.8 us -> 70.6 us (0.74)
  matrix products: 13.7 us -> 0 us
  Pallas kernels: 0 us -> 9.76 us
  blocking collectives: 31.4 us -> 23.2 us
  local copies, waits for them, and re-layouts: 10.7 us -> 3.1 us
  waiting for transfers between devices: 25.9 us -> 19.8 us
  starting transfers between devices: 9.15 us -> 13.4 us
  other arithmetic: 3.16 us -> 0.08 us
    all_to_all x1, waiting for transfers between devices: 25.9 us -> 0.01 us  [exchange(): return lax.all_to_all(t.reshape(ny, own, width), 'y', 0, 0, tiled=True)]
    ppermute x0 -> x2, waiting for transfers between devices: none -> 19.8 us  [swapped(): return lax.ppermute(t, 'z', swap)]
    dot_general x6 -> x0, matrix products: 13.7 us -> none  [the longest x4 11.5 us: attend(): jnp.einsum('apn,naf->paf', weight_matrices, value_head_blocks, preferred_...]
    pallas_call x0 -> x4, Pallas kernels: none -> 9.76 us  [the longest x1 7.28 us: layer(): pl.pallas_call(attend_kernel, out_shape=sds((ny * own, width)), in_specs=...]
    all_to_all x1, blocking collectives: 31.4 us -> 23.2 us  [exchange(): return lax.all_to_all(t.reshape(ny, own, width), 'y', 0, 0, tiled=True)]
    ppermute x0 -> x2, starting transfers between devices: none -> 6.2 us  [swapped(): return lax.ppermute(t, 'z', swap)]
    while x10 -> x0, local copies, waits for them, and re-layouts: 4.81 us -> none
    dynamic_update_slice x8 -> x0, local copies, waits for them, and re-layouts: 3.48 us -> none  [on_device(): lax.map(one_block, (every_query.reshape(blocks, block_rows, width), all_l...]
  transfers between devices with their start and end apart: 1 -> 3, of which waited for: 1 -> 2; matrix products, arithmetic and copies ran while one was open for 2% -> 1% of each run, Pallas kernels for 0% -> 0%
where the time goes in v1:
time: 70.6 us; the launch traced here: 70.2 us
  blocking collectives  23.2 us (33%)
  waiting for transfers between devices  19.8 us (28%)
  starting transfers between devices  13.4 us (19%)
  Pallas kernels  9.76 us (14%)
  local copies, waits for them, and re-layouts  3.1 us (4%)
  between operations  0.79 us (1%)
    all_to_all x1, blocking collectives, exchange(): return lax.all_to_all(t.reshape(ny, own, width), 'y', 0, 0, tiled=True)  23.2 us
    ppermute x2, waiting for transfers between devices, swapped(): return lax.ppermute(t, 'z', swap)  19.8 us
    pallas_call x1, Pallas kernels, layer(): pl.pallas_call(attend_kernel, out_shape=sds((ny * own, width)), in_specs=...  7.28 us
    all_to_all x1, starting transfers between devices, exchange(): return lax.all_to_all(t.reshape(ny, own, width), 'y', 0, 0, tiled=True)  7.23 us
    ppermute x2, starting transfers between devices, swapped(): return lax.ppermute(t, 'z', swap)  6.2 us
    unnamed x18, local copies, waits for them, and re-layouts  2.79 us
  transfers between devices with their start and end apart: 3, of which 2 were waited for; matrix products, arithmetic and copies ran while one was open for 1% of the time, Pallas kernels for 0%

profile of v1, /device:TPU:6, one launch (start us, length us, event | category | flops | bytes accessed | tf_op | source)
XLA Modules:
  0.0 70.2 jit_solution(6178833565058847360)
XLA Ops:
  0.0 0.0 copy-start
  0.0 1.2 %copy-done = bf16[512,1024]{1,0:T(8,128)(2,1)S(1)} copy-done((bf16[512,1024]{1,0:T(8,128)(2,1)S(1)}, bf16[512,1024]{1,0:T(8,128)(2,1)}, u32[]{:S(2)}) %copy-start) | copy-done | bytes 1048600
  1.2 0.0 copy-start.4
  1.2 0.8 %copy-done.4 = bf16[64,512]{1,0:T(8,128)(2,1)S(1)} copy-done((bf16[64,512]{1,0:T(8,128)(2,1)S(1)}, bf16[64,512]{1,0:T(8,128)(2,1)}, u32[]{:S(2)}) %copy-start.4) | copy-done | bytes 65560
  2.1 0.0 copy-start.6
  2.1 0.7 copy-done.6
  2.7 1.2 %project.1 = (bf16[8,64,512]{2,1,0:T(8,128)(2,1)}, f32[64,512]{1,0:T(8,128)S(1)}) custom-call(bf16[64,512]{1,0:T(8,128)(2,1)S(1)} %copy-done.4, f32[1,512]{1,0:T(1,128)S(1)} %bitcast.9, bf16[512,1024]{1,0:T(8,128)(2,1)S(1)} %copy-done), custom_call_target="tpu_custom_call" | custom-call | tf_op jit(solution)/shard_map/project/pallas_call | solution.py:93
  3.9 0.0 copy-start.8
  3.9 0.0 copy-start.1
  3.9 7.2 %all-to-all-start = ((bf16[8,64,512]{2,1,0:T(8,128)(2,1)}), bf16[8,64,512]{2,1,0:T(8,128)(2,1)S(1)}, u32[]{:S(2)}, u32[]{:S(2)}) async-start(bf16[8,64,512]{2,1,0:T(8,128)(2,1)} %get-tuple-element.7), calls=%async_computation | async-start | bytes 1048576 | tf_op jit(solution)/shard_map/all_to_all | solution.py:87
  11.2 0.0 copy-done.8
  11.2 0.0 copy-done.1
  11.2 0.0 copy-start.3
  11.2 0.3 scale.1.k0_ref
  11.5 4.3 %collective-permute-start = (bf16[512,512]{1,0:T(8,128)(2,1)S(1)}, bf16[512,512]{1,0:T(8,128)(2,1)S(1)}, u32[]{:S(2)}, u32[]{:S(2)}) collective-permute-start(bf16[512,512]{1,0:T(8,128)(2,1)S(1)} %scale.1.k0_ref), channel_id=1, source_target_pairs={{0,1},{1,0},{2,3},{3,2},{4,5},{5,4},{6,7},{7,6},{8,9},{9,8},{10,11... | collective-permute-start | bytes 1572872 | tf_op jit(solution)/shard_map/ppermute | solution.py:90
  15.8 0.0 copy-done.3
  15.8 1.9 %collective-permute-start.1 = (bf16[512,512]{1,0:T(8,128)(2,1)S(1)}, bf16[512,512]{1,0:T(8,128)(2,1)S(1)}, u32[]{:S(2)}, u32[]{:S(2)}) collective-permute-start(bf16[512,512]{1,0:T(8,128)(2,1)S(1)} %copy-done.3), channel_id=1, source_target_pairs={{0,1},{1,0},{2,3},{3,2},{4,5},{5,4},{6,7},{7,6},{8,9},{9,8},{10,11... | collective-permute-start | bytes 1572872 | tf_op jit(solution)/shard_map/ppermute | solution.py:90
  17.7 0.0 copy-start.7
  18.4 0.0 copy-done.7
  18.4 0.1 reshape.22
  18.5 0.2 reshape.25.lim_ref
  18.7 0.1 pad_add_fusion.off_ref
  18.8 9.7 %collective-permute-done.k1_ref = bf16[512,512]{1,0:T(8,128)(2,1)S(1)} collective-permute-done((bf16[512,512]{1,0:T(8,128)(2,1)S(1)}, bf16[512,512]{1,0:T(8,128)(2,1)S(1)}, u32[]{:S(2)}, u32[]{:S(2)}) %collective-permute-start) | collective-permute-done | bytes 524320 | tf_op jit(solution)/shard_map/ppermute | solution.py:90
  28.5 10.1 %collective-permute-done.1.v1_ref = bf16[512,512]{1,0:T(8,128)(2,1)S(1)} collective-permute-done((bf16[512,512]{1,0:T(8,128)(2,1)S(1)}, bf16[512,512]{1,0:T(8,128)(2,1)S(1)}, u32[]{:S(2)}, u32[]{:S(2)}) %collective-permute-start.1) | collective-permute-done | bytes 524320 | tf_op jit(solution)/shard_map/ppermute | solution.py:90
  38.6 0.0 all-to-all-done
  38.6 7.3 %attend.1 = bf16[512,512]{1,0:T(8,128)(2,1)S(1)} custom-call(s32[2]{0:T(128)S(1)} %pad_add_fusion.off_ref, bf16[512,512]{1,0:T(8,128)(2,1)S(1)} %bitcast.7, bf16[512,512]{1,0:T(8,128)(2,1)S(1)} %scale.1.k0_ref, bf16[512,512]{1,0:T(8,128)(2,1)S(1)} %copy-done.3, bf16[512,512]{1,0:T(8,128)(2,1)S(1)} %collective-permute-done.k1_ref, ...), custom_call_target="tpu_custom_call" | custom-call | tf_op jit(solution)/shard_map/attend/pallas_call | solution.py:109
  45.9 0.0 copy-start.2
  45.9 0.0 copy-start.5
  46.0 23.2 %all_to_all.10.t_ref = bf16[8,64,512]{2,1,0:T(8,128)(2,1)S(1)} all-to-all(bf16[8,64,512]{2,1,0:T(8,128)(2,1)S(1)} %bitcast.8), channel_id=1, replica_groups=mesh['users'=32,'y'=8,'z'=2] {'y'}, dimensions={0} | all-to-all | bytes 1048576 | tf_op jit(solution)/shard_map/all_to_all | solution.py:87
  69.2 0.0 copy-done.2
  69.2 0.0 copy-done.5
  69.2 1.0 %finish.1 = bf16[64,512]{1,0:T(8,128)(2,1)} custom-call(bf16[8,64,512]{2,1,0:T(8,128)(2,1)S(1)} %all_to_all.10.t_ref, f32[64,512]{1,0:T(8,128)S(1)} %get-tuple-element.8.gate_ref, bf16[64,512]{1,0:T(8,128)(2,1)S(1)} %copy-done.5, bf16[512,512]{1,0:T(8,128)(2,1)S(1)} %copy-done.2), custom_call_target="tpu_custom_call" | custom-call | tf_op jit(solution)/shard_map/finish/pallas_call | solution.py:114
  (3 shorter events, 0.0 us)
Async XLA Ops:
  0.0 1.2 %copy-start = (bf16[512,1024]{1,0:T(8,128)(2,1)S(1)}, bf16[512,1024]{1,0:T(8,128)(2,1)}, u32[]{:S(2)}) copy-start(bf16[512,1024]{1,0:T(8,128)(2,1)} %w_ref.2) | copy-start | bytes 3145732
  1.2 0.8 %copy-start.4 = (bf16[64,512]{1,0:T(8,128)(2,1)S(1)}, bf16[64,512]{1,0:T(8,128)(2,1)}, u32[]{:S(2)}) copy-start(bf16[64,512]{1,0:T(8,128)(2,1)} %x_ref.3) | copy-start | bytes 196612
  2.1 0.7 copy-start.6
  3.9 7.2 %copy-start.8 = (bf16[512]{0:T(512)(128)(2,1)S(1)}, bf16[512]{0:T(512)(128)(2,1)}, u32[]{:S(2)}) copy-start(bf16[512]{0:T(512)(128)(2,1)} %param.12) | copy-start | bytes 3076
  3.9 7.3 %copy-start.1 = (bf16[512,512]{1,0:T(8,128)(2,1)S(1)}, bf16[512,512]{1,0:T(8,128)(2,1)}, u32[]{:S(2)}) copy-start(bf16[512,512]{1,0:T(8,128)(2,1)} %k_ref.1) | copy-start | bytes 1572868
  3.9 34.7 %all-to-all-start = ((bf16[8,64,512]{2,1,0:T(8,128)(2,1)}), bf16[8,64,512]{2,1,0:T(8,128)(2,1)S(1)}, u32[]{:S(2)}, u32[]{:S(2)}) async-start(bf16[8,64,512]{2,1,0:T(8,128)(2,1)} %get-tuple-element.7), calls=%async_computation | async-start | bytes 1048576 | tf_op jit(solution)/shard_map/all_to_all | solution.py:87
  11.2 4.6 %copy-start.3 = (bf16[512,512]{1,0:T(8,128)(2,1)S(1)}, bf16[512,512]{1,0:T(8,128)(2,1)}, u32[]{:S(2)}) copy-start(bf16[512,512]{1,0:T(8,128)(2,1)} %v0_ref.1) | copy-start | bytes 1572868
  11.5 17.0 %collective-permute-start = (bf16[512,512]{1,0:T(8,128)(2,1)S(1)}, bf16[512,512]{1,0:T(8,128)(2,1)S(1)}, u32[]{:S(2)}, u32[]{:S(2)}) collective-permute-start(bf16[512,512]{1,0:T(8,128)(2,1)S(1)} %scale.1.k0_ref), channel_id=1, source_target_pairs={{0,1},{1,0},{2,3},{3,2},{4,5},{5,4},{6,7},{7,6},{8,9},{9,8},{10,11... | collective-permute-start | bytes 1572872 | tf_op jit(solution)/shard_map/ppermute | solution.py:90
  15.8 22.9 %collective-permute-start.1 = (bf16[512,512]{1,0:T(8,128)(2,1)S(1)}, bf16[512,512]{1,0:T(8,128)(2,1)S(1)}, u32[]{:S(2)}, u32[]{:S(2)}) collective-permute-start(bf16[512,512]{1,0:T(8,128)(2,1)S(1)} %copy-done.3), channel_id=1, source_target_pairs={{0,1},{1,0},{2,3},{3,2},{4,5},{5,4},{6,7},{7,6},{8,9},{9,8},{10,11... | collective-permute-start | bytes 1572872 | tf_op jit(solution)/shard_map/ppermute | solution.py:90
  17.7 0.7 copy-start.7
  45.9 23.2 %copy-start.2 = (bf16[512,512]{1,0:T(8,128)(2,1)S(1)}, bf16[512,512]{1,0:T(8,128)(2,1)}, u32[]{:S(2)}) copy-start(bf16[512,512]{1,0:T(8,128)(2,1)} %w_ref.3) | copy-start | bytes 1572868
  45.9 23.2 %copy-start.5 = (bf16[64,512]{1,0:T(8,128)(2,1)S(1)}, bf16[64,512]{1,0:T(8,128)(2,1)}, u32[]{:S(2)}) copy-start(bf16[64,512]{1,0:T(8,128)(2,1)} %x_ref.3) | copy-start | bytes 196612

commit v2 on v1

v2 whole, which is shorter than its diff:
```python
import jax
import jax.numpy as jnp
from jax import lax
from jax.experimental import pallas as pl
from jax.experimental.pallas import tpu as pltpu
from jax.sharding import Mesh, PartitionSpec as P


F32 = jnp.float32
BF16 = jnp.bfloat16
VM = pl.BlockSpec(memory_space=pltpu.VMEM)
HB = pl.BlockSpec(memory_space=pltpu.HBM)
SM = pl.BlockSpec(memory_space=pltpu.SMEM)
PARAMS = pltpu.CompilerParams(vmem_limit_bytes=40 * 1024 * 1024)


def center(v):
    mean = jnp.mean(v, axis=-1, keepdims=True)
    var = jnp.mean((v - mean) ** 2, axis=-1, keepdims=True)
    return (v - mean) / jnp.sqrt(var + 1e-5)


def project_kernel(x_hbm, gain_hbm, w_hbm, q_ref, x_ref, gain_ref, w_ref, sems):
    width = w_ref.shape[1]
    loads = [
        pltpu.make_async_copy(x_hbm, x_ref, sems.at[0]),
        pltpu.make_async_copy(gain_hbm, gain_ref, sems.at[1]),
        pltpu.make_async_copy(w_hbm.at[:, pl.ds(0, width)], w_ref, sems.at[2]),
    ]
    for load in loads:
        load.start()
    loads[0].wait()
    loads[1].wait()
    normed = (center(x_ref[...].astype(F32)) * gain_ref[...]).astype(BF16)
    loads[2].wait()
    p = jnp.dot(normed, w_ref[...], preferred_element_type=F32)
    q = (p / (1.0 + jnp.exp(-p))).astype(BF16)
    half = width // 2
    ny = q_ref.shape[1]
    for h in range(2):
        for i in range(ny):
            q_ref[h, i] = q[:, h * half:(h + 1) * half]


def gate_kernel(x_ref, gain_ref, w_ref, gate_ref):
    width = x_ref.shape[1]
    normed = (center(x_ref[...].astype(F32)) * gain_ref[...]).astype(BF16)
    p = jnp.dot(normed, w_ref[:, width:], preferred_element_type=F32)
    gate_ref[...] = p / (1.0 + jnp.exp(-p))


def pack_kernel(k_ref, v_ref, s_ref, o_ref):
    rows, width = k_ref.shape
    half = width // 2
    col = jnp.broadcast_to(s_ref[...].astype(F32) * (1.0 / 16.0), (8, rows)).T[:, :1]
    k = (k_ref[...].astype(F32) * col).astype(BF16)
    for h in range(2):
        o_ref[h, :rows] = k[:, h * half:(h + 1) * half]
        o_ref[h, rows:] = v_ref[:, h * half:(h + 1) * half]


def attend_part(q_ref, kv_ref, mask, cs):
    n = kv_ref.shape[0] // 2
    low = lax.broadcasted_iota(jnp.int32, (1, 128), 1) < 64
    q = q_ref[:, cs]
    k = kv_ref[:n, cs]
    v = kv_ref[n:, cs]
    weights = []
    values = []
    for sel in (low, jnp.logical_not(low)):
        head = jnp.where(sel, q, jnp.zeros_like(q))
        u = lax.dot_general(head, k, (((1,), (1,)), ((), ())), preferred_element_type=F32)
        weights.append((u * (1.0 + jnp.tanh(u))).astype(BF16) * mask)
        values.append(jnp.where(sel, v, jnp.zeros_like(v)))
    return jnp.dot(jnp.concatenate(weights, 1), jnp.concatenate(values, 0), preferred_element_type=F32)


def seen(off, lim_ref, n):
    pos = lax.broadcasted_iota(jnp.int32, (lim_ref.shape[0], n), 1) + off
    return jnp.where(pos < lim_ref[...], 1.0, 0.0).astype(BF16)


def near_kernel(off_ref, q_ref, kv_ref, lim_ref, o_ref):
    mask = seen(off_ref[0], lim_ref, kv_ref.shape[0] // 2)
    for pair in range(q_ref.shape[1] // 128):
        cs = slice(pair * 128, (pair + 1) * 128)
        o_ref[:, cs] = attend_part(q_ref, kv_ref, mask, cs)


def far_kernel(off_ref, q_ref, kv_ref, lim_ref, near_ref, o_ref):
    mask = seen(off_ref[1], lim_ref, kv_ref.shape[0] // 2)
    for pair in range(q_ref.shape[1] // 128):
        cs = slice(pair * 128, (pair + 1) * 128)
        o_ref[:, cs] = (near_ref[:, cs] + attend_part(q_ref, kv_ref, mask, cs)).astype(BF16)


def finish_kernel(t_ref, gate_ref, x_ref, w_ref, o_ref):
    sides = [jnp.sum(t_ref[h].astype(F32), axis=0) for h in range(2)]
    total = jnp.concatenate(sides, axis=1)
    mixed = (center(total) * gate_ref[...]).astype(BF16)
    o_ref[...] = (x_ref[...].astype(F32) + jnp.dot(mixed, w_ref[...], preferred_element_type=F32)).astype(BF16)


def sds(shape, dtype=BF16):
    return jax.ShapeDtypeStruct(shape, dtype)


def layer(cand_x, hist_keys, hist_values, key_scale, hist_len, cand_limit, ln_gain, w_qu, w_out):
    own, width = cand_x.shape
    n = hist_keys.shape[0]
    half = width // 2
    ny = lax.axis_size("y")
    nz = lax.axis_size("z")
    y = lax.axis_index("y")
    z = lax.axis_index("z")
    swap = [(i, 1 - i) for i in range(nz)]
    def exchange(t):
        return lax.all_to_all(t.reshape(nz * ny, own, half), ("z", "y"), 0, 0, tiled=True)

    gain = ln_gain.reshape(1, width)
    q = pl.pallas_call(
        project_kernel, out_shape=sds((nz, ny, own, half)), in_specs=[HB] * 3, out_specs=VM,
        scratch_shapes=[
            pltpu.VMEM((own, width), BF16), pltpu.VMEM((1, width), F32), pltpu.VMEM((width, width), BF16),
            pltpu.SemaphoreType.DMA((3,)),
        ],
        compiler_params=PARAMS, name="project",
    )(*(pltpu.with_memory_space_constraint(v, pltpu.HBM) for v in (cand_x, gain, w_qu)))
    gate = pl.pallas_call(
        gate_kernel, out_shape=sds((own, width), F32), in_specs=[VM] * 3, out_specs=VM,
        compiler_params=PARAMS, name="gate",
    )(cand_x, gain, w_qu)
    every_q = exchange(q).reshape(nz * ny * own, half)
    kv = pl.pallas_call(
        pack_kernel, out_shape=sds((nz, 2 * n, half)), in_specs=[VM] * 3, out_specs=VM,
        compiler_params=PARAMS, name="pack",
    )(hist_keys, hist_values, key_scale.reshape(1, n))
    kv_own = lax.dynamic_index_in_dim(kv, z, 0, keepdims=False)
    kv_out = lax.dynamic_index_in_dim(kv, 1 - z, 0, keepdims=False)
    kv_far = lax.ppermute(kv_out, "z", swap)

    limits = jnp.minimum(cand_limit, hist_len[0]).reshape(ny, nz, own)
    limits = jnp.swapaxes(limits, 0, 1).reshape(nz * ny * own, 1)
    offsets = jnp.stack([(y * nz + z) * n, (y * nz + 1 - z) * n]).astype(jnp.int32)

    near = pl.pallas_call(
        near_kernel, out_shape=sds((nz * ny * own, half), F32), in_specs=[SM] + [VM] * 3, out_specs=VM,
        compiler_params=PARAMS, name="near",
    )(offsets, every_q, kv_own, limits)
    outs = pl.pallas_call(
        far_kernel, out_shape=sds((nz * ny * own, half)), in_specs=[SM] + [VM] * 4, out_specs=VM,
        compiler_params=PARAMS, name="far",
    )(offsets, every_q, kv_far, limits, near)
    totals = exchange(outs).reshape(nz, ny, own, half)
    return pl.pallas_call(
        finish_kernel, out_shape=sds((own, width)), in_specs=[VM] * 4, out_specs=VM,
        compiler_params=PARAMS, name="finish",
    )(totals, gate, cand_x, w_out)


def solution(mesh):
    users, hist = mesh.devices.shape
    grid = Mesh(mesh.devices.reshape(users, hist // 2, 2), ("users", "y", "z"))
    both = ("users", "y", "z")
    in_specs = (P(both, None), P(both, None), P(both, None), P(both), P("users"), P("users"), P(), P(), P())
    return jax.shard_map(layer, mesh=grid, in_specs=in_specs, out_specs=P(both, None), check_vma=False)
```

time: 70.6 us -> 58.7 us (0.83)
  blocking collectives: 23.2 us -> 0 us
  starting transfers between devices: 13.4 us -> 19.8 us
  waiting for transfers between devices: 19.8 us -> 25 us
  local copies, waits for them, and re-layouts: 3.1 us -> 1.36 us
  Pallas kernels: 9.76 us -> 10.8 us
    all_to_all x1 -> x0, blocking collectives: 23.2 us -> none  [exchange(): return lax.all_to_all(t.reshape(ny, own, width), 'y', 0, 0, tiled=True)]
    all_to_all x1 -> x2, waiting for transfers between devices: 0.01 us -> 23.2 us  [exchange(): lax.all_to_all(t.reshape(nz * ny, own, half), ('z', 'y'), 0, 0, tiled=True)]
    ppermute x2 -> x1, waiting for transfers between devices: 19.8 us -> 1.81 us  [layer(): kv_far = lax.ppermute(kv_out, 'z', swap)]
    all_to_all x1 -> x2, starting transfers between devices: 7.23 us -> 16 us  [exchange(): lax.all_to_all(t.reshape(nz * ny, own, half), ('z', 'y'), 0, 0, tiled=True)]
    ppermute x2 -> x1, starting transfers between devices: 6.2 us -> 3.83 us  [layer(): kv_far = lax.ppermute(kv_out, 'z', swap)]
    unnamed x18 -> x16, local copies, waits for them, and re-layouts: 2.79 us -> 0.73 us
    pallas_call x3 -> x5, Pallas kernels: 8.74 us -> 9.82 us  [the longest x1 3.91 us: layer(): pl.pallas_call(far_kernel, out_shape=sds((nz * ny * own, half)), in_specs...]
  transfers between devices with their start and end apart: 3 -> 3, of which waited for: 2 -> 3; matrix products, arithmetic and copies ran while one was open for 1% -> 1% of each run, Pallas kernels for 0% -> 6%
where the time goes in v2:
time: 58.7 us; the launch traced here: 57.9 us
  waiting for transfers between devices  25 us (43%)
  starting transfers between devices  19.8 us (34%)
  Pallas kernels  10.8 us (18%)
  local copies, waits for them, and re-layouts  1.36 us (2%)
  between operations  0.82 us (1%)
    all_to_all x2, waiting for transfers between devices, exchange(): lax.all_to_all(t.reshape(nz * ny, own, half), ('z', 'y'), 0, 0, tiled=True)  23.2 us
    all_to_all x2, starting transfers between devices, exchange(): lax.all_to_all(t.reshape(nz * ny, own, half), ('z', 'y'), 0, 0, tiled=True)  16 us
    pallas_call x1, Pallas kernels, layer(): pl.pallas_call(far_kernel, out_shape=sds((nz * ny * own, half)), in_specs...  3.91 us
    ppermute x1, starting transfers between devices, layer(): kv_far = lax.ppermute(kv_out, 'z', swap)  3.83 us
    pallas_call x1, Pallas kernels, layer(): pl.pallas_call(near_kernel, out_shape=sds((nz * ny * own, half), F32), in...  3.07 us
    pallas_call x1, Pallas kernels, layer(): pl.pallas_call(project_kernel, out_shape=sds((nz, ny, own, half)), in_spe...  2.18 us
    ppermute x1, waiting for transfers between devices, layer(): kv_far = lax.ppermute(kv_out, 'z', swap)  1.81 us
  transfers between devices with their start and end apart: 3, of which 3 were waited for; matrix products, arithmetic and copies ran while one was open for 1% of the time, Pallas kernels for 6%

profile of v2, /device:TPU:6, one launch (start us, length us, event | category | flops | bytes accessed | tf_op | source)
XLA Modules:
  0.0 57.9 jit_solution(16272217943590426235)
XLA Ops:
  0.0 2.2 %project.1 = bf16[2,8,64,256]{3,2,1,0:T(8,128)(2,1)} custom-call(bf16[64,512]{1,0:T(8,128)(2,1)} %x_ref.3, f32[1,512]{1,0:T(1,128)} %bitcast.17, bf16[512,1024]{1,0:T(8,128)(2,1)} %w_ref.2), custom_call_target="tpu_custom_call" | custom-call | tf_op jit(solution)/shard_map/project/pallas_call | solution.py:121
  2.2 0.0 copy-start.2
  2.2 0.0 copy-start.3
  2.2 9.2 %all-to-all-start = ((bf16[16,64,256]{2,1,0:T(8,128)(2,1)}), bf16[16,64,256]{2,1,0:T(8,128)(2,1)S(1)}, u32[]{:S(2)}, u32[]{:S(2)}) async-start(bf16[16,64,256]{2,1,0:T(8,128)(2,1)} %bitcast.3), calls=%async_computation | async-start | bytes 1048576 | tf_op jit(solution)/shard_map/all_to_all | solution.py:118
  11.4 0.0 copy-start.7
  11.4 0.7 %copy-done.7 = bf16[512]{0:T(512)(128)(2,1)S(1)} copy-done((bf16[512]{0:T(512)(128)(2,1)S(1)}, bf16[512]{0:T(512)(128)(2,1)}, u32[]{:S(2)}) %copy-start.7) | copy-done | bytes 1048
  12.1 0.0 copy-done.2
  12.1 0.0 copy-done.3
  12.1 0.3 pack.1
  12.4 0.1 dynamic-slice_bitcast_fusion
  12.4 3.8 %collective-permute-start = (bf16[1024,256]{1,0:T(8,128)(2,1)S(1)}, bf16[1024,256]{1,0:T(8,128)(2,1)S(1)}, u32[]{:S(2)}, u32[]{:S(2)}) collective-permute-start(bf16[1024,256]{1,0:T(8,128)(2,1)S(1)} %get-tuple-element.6), channel_id=1, source_target_pairs={{0,1},{1,0},{2,3},{3,2},{4,5},{5,4},{6,7},{7,6},{8,9},{9,8},{10,11... | collective-permute-start | bytes 1572872 | tf_op jit(solution)/shard_map/ppermute | solution.py:140
  16.3 0.0 copy-start.6
  17.0 0.0 copy-done.6
  17.0 0.1 reshape.28
  17.1 0.5 reshape.32.lim_ref
  17.6 0.1 pad_add_fusion.off_ref
  17.6 9.4 %all-to-all-done = bf16[16,64,256]{2,1,0:T(8,128)(2,1)S(1)} async-done(((bf16[16,64,256]{2,1,0:T(8,128)(2,1)}), bf16[16,64,256]{2,1,0:T(8,128)(2,1)S(1)}, u32[]{:S(2)}, u32[]{:S(2)}) %all-to-all-start) | async-done | bytes 524320 | tf_op jit(solution)/shard_map/all_to_all | solution.py:118
  27.1 3.1 %near.1.near_ref = f32[1024,256]{1,0:T(8,128)S(1)} custom-call(s32[2]{0:T(128)S(1)} %pad_add_fusion.off_ref, bf16[1024,256]{1,0:T(8,128)(2,1)S(1)} %bitcast.14, bf16[1024,256]{1,0:T(8,128)(2,1)S(1)} %get-tuple-element.5.kv_ref, s32[1024,1]{1,0:T(8,128)S(1)} %reshape.32.lim_ref), custom_call_target="tpu_custom_call" | custom-call | tf_op jit(solution)/shard_map/near/pallas_call | solution.py:146
  30.1 1.8 %collective-permute-done.kv_ref = bf16[1024,256]{1,0:T(8,128)(2,1)S(1)} collective-permute-done((bf16[1024,256]{1,0:T(8,128)(2,1)S(1)}, bf16[1024,256]{1,0:T(8,128)(2,1)S(1)}, u32[]{:S(2)}, u32[]{:S(2)}) %collective-permute-start) | collective-permute-done | bytes 524320 | tf_op jit(solution)/shard_map/ppermute | solution.py:140
  31.9 0.0 copy-start.1
  31.9 0.0 copy-start.5
  31.9 3.9 %far.1 = bf16[1024,256]{1,0:T(8,128)(2,1)} custom-call(s32[2]{0:T(128)S(1)} %pad_add_fusion.off_ref, bf16[1024,256]{1,0:T(8,128)(2,1)S(1)} %bitcast.15, bf16[1024,256]{1,0:T(8,128)(2,1)S(1)} %collective-permute-done.kv_ref, s32[1024,1]{1,0:T(8,128)S(1)} %reshape.32.lim_ref, f32[1024,256]{1,0:T(8,128)S(1)} %near.1.near_ref), custom_call_target="tpu_custom_call" | custom-call | tf_op jit(solution)/shard_map/far/pallas_call | solution.py:150
  35.9 0.0 copy-start
  35.9 6.8 %all-to-all-start.1 = ((bf16[16,64,256]{2,1,0:T(8,128)(2,1)}), bf16[16,64,256]{2,1,0:T(8,128)(2,1)S(1)}, u32[]{:S(2)}, u32[]{:S(2)}) async-start(bf16[16,64,256]{2,1,0:T(8,128)(2,1)} %bitcast.9), calls=%async_computation.1 | async-start | bytes 1048576 | tf_op jit(solution)/shard_map/all_to_all | solution.py:118
  42.7 0.0 copy-done.1
  42.7 0.0 copy-done.5
  42.7 0.0 copy-done
  42.7 0.0 copy-start.4
  42.7 0.4 gate.1.gate_ref
  43.1 13.7 %all-to-all-done.1 = bf16[16,64,256]{2,1,0:T(8,128)(2,1)S(1)} async-done(((bf16[16,64,256]{2,1,0:T(8,128)(2,1)}), bf16[16,64,256]{2,1,0:T(8,128)(2,1)S(1)}, u32[]{:S(2)}, u32[]{:S(2)}) %all-to-all-start.1) | async-done | bytes 524320 | tf_op jit(solution)/shard_map/all_to_all | solution.py:118
  56.9 0.0 copy-done.4
  56.9 1.0 %finish.1 = bf16[64,512]{1,0:T(8,128)(2,1)} custom-call(bf16[2,8,64,256]{3,2,1,0:T(8,128)(2,1)S(1)} %bitcast.16, f32[64,512]{1,0:T(8,128)S(1)} %gate.1.gate_ref, bf16[64,512]{1,0:T(8,128)(2,1)S(1)} %copy-done.1, bf16[512,512]{1,0:T(8,128)(2,1)S(1)} %copy-done.4), custom_call_target="tpu_custom_call" | custom-call | tf_op jit(solution)/shard_map/finish/pallas_call | solution.py:155
  (3 shorter events, 0.0 us)
Async XLA Ops:
  2.2 9.9 %copy-start.2 = (bf16[512,512]{1,0:T(8,128)(2,1)S(1)}, bf16[512,512]{1,0:T(8,128)(2,1)}, u32[]{:S(2)}) copy-start(bf16[512,512]{1,0:T(8,128)(2,1)} %k_ref.1) | copy-start | bytes 1572868
  2.2 9.9 %copy-start.3 = (bf16[512,512]{1,0:T(8,128)(2,1)S(1)}, bf16[512,512]{1,0:T(8,128)(2,1)}, u32[]{:S(2)}) copy-start(bf16[512,512]{1,0:T(8,128)(2,1)} %v_ref.1) | copy-start | bytes 1572868
  2.2 24.8 %all-to-all-start = ((bf16[16,64,256]{2,1,0:T(8,128)(2,1)}), bf16[16,64,256]{2,1,0:T(8,128)(2,1)S(1)}, u32[]{:S(2)}, u32[]{:S(2)}) async-start(bf16[16,64,256]{2,1,0:T(8,128)(2,1)} %bitcast.3), calls=%async_computation | async-start | bytes 1048576 | tf_op jit(solution)/shard_map/all_to_all | solution.py:118
  11.4 0.7 %copy-start.7 = (bf16[512]{0:T(512)(128)(2,1)S(1)}, bf16[512]{0:T(512)(128)(2,1)}, u32[]{:S(2)}) copy-start(bf16[512]{0:T(512)(128)(2,1)} %param.12) | copy-start | bytes 3076
  12.4 19.5 %collective-permute-start = (bf16[1024,256]{1,0:T(8,128)(2,1)S(1)}, bf16[1024,256]{1,0:T(8,128)(2,1)S(1)}, u32[]{:S(2)}, u32[]{:S(2)}) collective-permute-start(bf16[1024,256]{1,0:T(8,128)(2,1)S(1)} %get-tuple-element.6), channel_id=1, source_target_pairs={{0,1},{1,0},{2,3},{3,2},{4,5},{5,4},{6,7},{7,6},{8,9},{9,8},{10,11... | collective-permute-start | bytes 1572872 | tf_op jit(solution)/shard_map/ppermute | solution.py:140
  16.3 0.7 %copy-start.6 = (s32[1024]{0:T(1024)S(1)}, s32[1024]{0:T(1024)}, u32[]{:S(2)}) copy-start(s32[1024]{0:T(1024)} %param.14) | copy-start | bytes 12292
  31.9 10.8 %copy-start.1 = (bf16[64,512]{1,0:T(8,128)(2,1)S(1)}, bf16[64,512]{1,0:T(8,128)(2,1)}, u32[]{:S(2)}) copy-start(bf16[64,512]{1,0:T(8,128)(2,1)} %x_ref.3) | copy-start | bytes 196612
  31.9 10.8 %copy-start.5 = (f32[512]{0:T(512)S(1)}, f32[512]{0:T(512)}, u32[]{:S(2)}) copy-start(f32[512]{0:T(512)} %param.15) | copy-start | bytes 6148
  35.9 6.9 %copy-start = (bf16[512,1024]{1,0:T(8,128)(2,1)S(1)}, bf16[512,1024]{1,0:T(8,128)(2,1)}, u32[]{:S(2)}) copy-start(bf16[512,1024]{1,0:T(8,128)(2,1)} %w_ref.2) | copy-start | bytes 3145732
  35.9 21.0 %all-to-all-start.1 = ((bf16[16,64,256]{2,1,0:T(8,128)(2,1)}), bf16[16,64,256]{2,1,0:T(8,128)(2,1)S(1)}, u32[]{:S(2)}, u32[]{:S(2)}) async-start(bf16[16,64,256]{2,1,0:T(8,128)(2,1)} %bitcast.9), calls=%async_computation.1 | async-start | bytes 1048576 | tf_op jit(solution)/shard_map/all_to_all | solution.py:118
  42.7 14.1 %copy-start.4 = (bf16[512,512]{1,0:T(8,128)(2,1)S(1)}, bf16[512,512]{1,0:T(8,128)(2,1)}, u32[]{:S(2)}) copy-start(bf16[512,512]{1,0:T(8,128)(2,1)} %w_ref.3) | copy-start | bytes 1572868

commit v3 on v2

v3 whole, which is shorter than its diff:
```python
import jax
import jax.numpy as jnp
from jax import lax
from jax.experimental import pallas as pl
from jax.experimental.pallas import tpu as pltpu
from jax.sharding import Mesh, PartitionSpec as P


F32 = jnp.float32
BF16 = jnp.bfloat16
VM = pl.BlockSpec(memory_space=pltpu.VMEM)
HB = pl.BlockSpec(memory_space=pltpu.HBM)
SM = pl.BlockSpec(memory_space=pltpu.SMEM)
PARAMS = pltpu.CompilerParams(vmem_limit_bytes=40 * 1024 * 1024)


def center(v):
    mean = jnp.mean(v, axis=-1, keepdims=True)
    var = jnp.mean((v - mean) ** 2, axis=-1, keepdims=True)
    return (v - mean) / jnp.sqrt(var + 1e-5)


def project_kernel(x_hbm, gain_hbm, w_hbm, q_ref, x_ref, gain_ref, w_ref, sems):
    width = w_ref.shape[1]
    loads = [
        pltpu.make_async_copy(x_hbm, x_ref, sems.at[0]),
        pltpu.make_async_copy(gain_hbm, gain_ref, sems.at[1]),
        pltpu.make_async_copy(w_hbm.at[:, pl.ds(0, width)], w_ref, sems.at[2]),
    ]
    for load in loads:
        load.start()
    loads[0].wait()
    loads[1].wait()
    normed = (center(x_ref[...].astype(F32)) * gain_ref[...]).astype(BF16)
    loads[2].wait()
    p = jnp.dot(normed, w_ref[...], preferred_element_type=F32)
    q = (p / (1.0 + jnp.exp(-p))).astype(BF16)
    parts, copies, _, part = q_ref.shape
    for h in range(parts):
        for i in range(copies):
            q_ref[h, i] = q[:, h * part:(h + 1) * part]


def gate_kernel(x_ref, gain_ref, w_ref, gate_ref):
    width = x_ref.shape[1]
    normed = (center(x_ref[...].astype(F32)) * gain_ref[...]).astype(BF16)
    p = jnp.dot(normed, w_ref[:, width:], preferred_element_type=F32)
    gate_ref[...] = p / (1.0 + jnp.exp(-p))


def pack_kernel(part_ref, k_ref, v_ref, s_ref, *outs):
    rows, width = k_ref.shape
    part = width // len(outs)
    col = jnp.broadcast_to(s_ref[...].astype(F32).reshape(1, rows) * (1.0 / 16.0), (8, rows)).T[:, :1]
    k = (k_ref[...].astype(F32) * col).astype(BF16)
    for h in range(len(outs)):

        @pl.when(part_ref[0] == h)
        def _():
            for flip, out in enumerate(outs):
                cs = slice((h ^ flip) * part, ((h ^ flip) + 1) * part)
                out[:rows] = k[:, cs]
                out[rows:] = v_ref[:, cs]


def attend_pair(q, parts, cs):
    low = lax.broadcasted_iota(jnp.int32, (1, 128), 1) < 64
    weights = []
    values = []
    for kv_ref, mask in parts:
        n = kv_ref.shape[0] // 2
        k = kv_ref[:n, cs]
        v = kv_ref[n:, cs]
        for sel in (low, jnp.logical_not(low)):
            head = jnp.where(sel, q, jnp.zeros_like(q))
            u = lax.dot_general(head, k, (((1,), (1,)), ((), ())), preferred_element_type=F32)
            weights.append((u * (1.0 + jnp.tanh(u))).astype(BF16) * mask)
            values.append(jnp.where(sel, v, jnp.zeros_like(v)))
    return jnp.dot(jnp.concatenate(weights, 1), jnp.concatenate(values, 0), preferred_element_type=F32)


def seen(off, lim_ref, kv_ref):
    pos = lax.broadcasted_iota(jnp.int32, (lim_ref.shape[0], kv_ref.shape[0] // 2), 1) + off
    return jnp.where(pos < lim_ref[...], 1.0, 0.0).astype(BF16)


def near_kernel(off_ref, q_ref, own_ref, side_ref, lim_ref, o_ref):
    parts = [(ref, seen(off_ref[i], lim_ref, ref)) for i, ref in enumerate((own_ref, side_ref))]
    o_ref[...] = attend_pair(q_ref[...], parts, slice(None))


def far_kernel(off_ref, q_ref, side_ref, both_ref, lim_ref, near_ref, o_ref):
    parts = [(ref, seen(off_ref[2 + i], lim_ref, ref)) for i, ref in enumerate((side_ref, both_ref))]
    o_ref[...] = (near_ref[...] + attend_pair(q_ref[...], parts, slice(None))).astype(BF16)


def finish_kernel(t_ref, gate_ref, x_ref, w_ref, o_ref):
    sides = [jnp.sum(t_ref[h].astype(F32), axis=0) for h in range(t_ref.shape[0])]
    total = jnp.concatenate(sides, axis=1)
    mixed = (center(total) * gate_ref[...]).astype(BF16)
    o_ref[...] = (x_ref[...].astype(F32) + jnp.dot(mixed, w_ref[...], preferred_element_type=F32)).astype(BF16)


def sds(shape, dtype=BF16):
    return jax.ShapeDtypeStruct(shape, dtype)


def layer(cand_x, hist_keys, hist_values, key_scale, hist_len, cand_limit, ln_gain, w_qu, w_out):
    own, width = cand_x.shape
    n = hist_keys.shape[0]
    pairs = lax.axis_size("pair")
    pair = lax.axis_index("pair")
    side = lax.axis_index("side")
    z = lax.axis_index("z")
    part = width // 4
    rows = 4 * pairs * own

    def exchange(t):
        return lax.all_to_all(t.reshape(4 * pairs, own, part), ("z", "side", "pair"), 0, 0, tiled=True)

    gain = ln_gain.reshape(1, width)
    q = pl.pallas_call(
        project_kernel, out_shape=sds((4, pairs, own, part)), in_specs=[HB] * 3, out_specs=VM,
        scratch_shapes=[
            pltpu.VMEM((own, width), BF16), pltpu.VMEM((1, width), F32), pltpu.VMEM((width, width), BF16),
            pltpu.SemaphoreType.DMA((3,)),
        ],
        compiler_params=PARAMS, name="project",
    )(*(pltpu.with_memory_space_constraint(v, pltpu.HBM) for v in (cand_x, gain, w_qu)))
    gate = pl.pallas_call(
        gate_kernel, out_shape=sds((own, width), F32), in_specs=[VM] * 3, out_specs=VM,
        compiler_params=PARAMS, name="gate",
    )(cand_x, gain, w_qu)
    every_q = exchange(q).reshape(rows, part)
    own_kv, to_side, to_z, to_both = pl.pallas_call(
        pack_kernel, out_shape=(sds((2 * n, part)),) * 4,
        in_specs=[SM] + [VM] * 3, out_specs=(VM,) * 4, compiler_params=PARAMS, name="pack",
    )((z * 2 + side).astype(jnp.int32).reshape(1), hist_keys, hist_values, key_scale)
    z_kv = lax.ppermute(to_z, "z", [(0, 1), (1, 0)])
    both_kv = lax.ppermute(to_both, ("side", "z"), [(i, 3 - i) for i in range(4)])
    side_kv = lax.ppermute(to_side, "side", [(0, 1), (1, 0)])

    limits = jnp.minimum(cand_limit, hist_len[0]).reshape(pairs, 2, 2, own)
    limits = jnp.transpose(limits, (2, 1, 0, 3)).reshape(rows, 1)
    offsets = jnp.stack(
        [((pair * 2 + s) * 2 + t) * n for s, t in ((side, z), (1 - side, 1 - z), (side, 1 - z), (1 - side, z))]
    ).astype(jnp.int32)

    total = pl.pallas_call(
        near_kernel, out_shape=sds((rows, part), F32), in_specs=[SM] + [VM] * 4, out_specs=VM,
        compiler_params=PARAMS, name="near",
    )(offsets, every_q, own_kv, both_kv, limits)
    total = pl.pallas_call(
        far_kernel, out_shape=sds((rows, part)), in_specs=[SM] + [VM] * 5, out_specs=VM,
        compiler_params=PARAMS, name="far",
    )(offsets, every_q, z_kv, side_kv, limits, total)
    totals = exchange(total).reshape(4, pairs, own, part)
    return pl.pallas_call(
        finish_kernel, out_shape=sds((own, width)), in_specs=[VM] * 4, out_specs=VM,
        compiler_params=PARAMS, name="finish",
    )(totals, gate, cand_x, w_out)


def solution(mesh):
    users, hist = mesh.devices.shape
    grid = Mesh(mesh.devices.reshape(users, hist // 4, 2, 2), ("users", "pair", "side", "z"))
    both = ("users", "pair", "side", "z")
    in_specs = (P(both, None), P(both, None), P(both, None), P(both), P("users"), P("users"), P(), P(), P())
    return jax.shard_map(layer, mesh=grid, in_specs=in_specs, out_specs=P(both, None), check_vma=False)
```

time: 58.7 us -> 56.9 us (0.969)
  waiting for transfers between devices: 25 us -> 17.5 us
  starting transfers between devices: 19.8 us -> 25.8 us
    all_to_all x2, waiting for transfers between devices: 23.2 us -> 9.25 us  [exchange(): lax.all_to_all(t.reshape(4 * pairs, own, part), ('z', 'side', 'pair'), 0,...]
    ppermute x1 -> x3, waiting for transfers between devices: 1.81 us -> 8.29 us  [the longest x1 8.29 us: layer(): lax.ppermute(to_both, ('side', 'z'), [(i, 3 - i) for i in range(4)])]
    ppermute x1 -> x3, starting transfers between devices: 3.83 us -> 9.21 us  [the longest x1 3.83 us: layer(): z_kv = lax.ppermute(to_z, 'z', [(0, 1), (1, 0)])]
    all_to_all x2, starting transfers between devices: 16 us -> 16.6 us  [exchange(): lax.all_to_all(t.reshape(4 * pairs, own, part), ('z', 'side', 'pair'), 0,...]
  transfers between devices with their start and end apart: 3 -> 5, of which waited for: 3 -> 2; matrix products, arithmetic and copies ran while one was open for 1% -> 1% of each run, Pallas kernels for 6% -> 7%
where the time goes in v3:
time: 56.9 us; the launch traced here: 56.4 us
  starting transfers between devices  25.8 us (45%)
  waiting for transfers between devices  17.5 us (31%)
  Pallas kernels  10.8 us (19%)
  local copies, waits for them, and re-layouts  1.27 us (2%)
  between operations  0.87 us (2%)
    all_to_all x2, starting transfers between devices, exchange(): lax.all_to_all(t.reshape(4 * pairs, own, part), ('z', 'side', 'pair'), 0,...  16.6 us
    all_to_all x2, waiting for transfers between devices, exchange(): lax.all_to_all(t.reshape(4 * pairs, own, part), ('z', 'side', 'pair'), 0,...  9.25 us
    ppermute x1, waiting for transfers between devices, layer(): lax.ppermute(to_both, ('side', 'z'), [(i, 3 - i) for i in range(4)])  8.29 us
    pallas_call x1, Pallas kernels, layer(): pl.pallas_call(far_kernel, out_shape=sds((rows, part)), in_specs=[SM] + [...  3.86 us
    ppermute x1, starting transfers between devices, layer(): z_kv = lax.ppermute(to_z, 'z', [(0, 1), (1, 0)])  3.83 us
    ppermute x1, starting transfers between devices, layer(): side_kv = lax.ppermute(to_side, 'side', [(0, 1), (1, 0)])  3.37 us
    pallas_call x1, Pallas kernels, layer(): pl.pallas_call(near_kernel, out_shape=sds((rows, part), F32), in_specs=[S...  2.99 us
    pallas_call x1, Pallas kernels, layer(): pl.pallas_call(project_kernel, out_shape=sds((4, pairs, own, part)), in_s...  2.12 us
  transfers between devices with their start and end apart: 5, of which 2 were waited for; matrix products, arithmetic and copies ran while one was open for 1% of the time, Pallas kernels for 7%

profile of v3, /device:TPU:6, one launch (start us, length us, event | category | flops | bytes accessed | tf_op | source)
XLA Modules:
  0.0 56.4 jit_solution(3052144910958686233)
XLA Ops:
  0.0 0.0 copy-start.3
  0.0 2.1 %project.1 = bf16[4,4,64,128]{3,2,1,0:T(8,128)(2,1)} custom-call(bf16[64,512]{1,0:T(8,128)(2,1)} %x_ref.3, f32[1,512]{1,0:T(1,128)} %bitcast.16, bf16[512,1024]{1,0:T(8,128)(2,1)} %w_ref.2), custom_call_target="tpu_custom_call" | custom-call | tf_op jit(solution)/shard_map/project/pallas_call | solution.py:122
  2.1 0.0 copy-start.2
  2.1 9.2 %all-to-all-start = ((bf16[16,64,128]{2,1,0:T(8,128)(2,1)}), bf16[16,64,128]{2,1,0:T(8,128)(2,1)S(1)}, u32[]{:S(2)}, u32[]{:S(2)}) async-start(bf16[16,64,128]{2,1,0:T(8,128)(2,1)} %bitcast.5), calls=%async_computation | async-start | bytes 524288 | tf_op jit(solution)/shard_map/all_to_all | solution.py:119
  11.3 0.0 copy-start.6
  11.3 0.0 copy-done.3
  11.3 0.0 copy-done.2
  11.4 0.7 %copy-done.6 = bf16[512]{0:T(512)(128)(2,1)S(1)} copy-done((bf16[512]{0:T(512)(128)(2,1)S(1)}, bf16[512]{0:T(512)(128)(2,1)}, u32[]{:S(2)}) %copy-start.6) | copy-done | bytes 1048
  12.0 0.4 pack.1
  12.4 3.8 %collective-permute-start = (bf16[1024,128]{1,0:T(8,128)(2,1)S(1)}, bf16[1024,128]{1,0:T(8,128)(2,1)S(1)}, u32[]{:S(2)}, u32[]{:S(2)}) collective-permute-start(bf16[1024,128]{1,0:T(8,128)(2,1)S(1)} %get-tuple-element.9), channel_id=1, source_target_pairs={{0,1},{1,0},{2,3},{3,2},{4,5},{5,4},{6,7},{7,6},{8,9},{9,8},{10,11... | collective-permute-start | bytes 786440 | tf_op jit(solution)/shard_map/ppermute | solution.py:139
  16.3 3.4 %collective-permute-start.1 = (bf16[1024,128]{1,0:T(8,128)(2,1)S(1)}, bf16[1024,128]{1,0:T(8,128)(2,1)S(1)}, u32[]{:S(2)}, u32[]{:S(2)}) collective-permute-start(bf16[1024,128]{1,0:T(8,128)(2,1)S(1)} %get-tuple-element.10), channel_id=1, source_target_pairs={{0,2},{2,0},{1,3},{3,1},{4,6},{6,4},{5,7},{7,5},{8,10},{10,8},{9,1... | collective-permute-start | bytes 786440 | tf_op jit(solution)/shard_map/ppermute | solution.py:141
  19.6 2.0 %collective-permute-start.2 = (bf16[1024,128]{1,0:T(8,128)(2,1)S(1)}, bf16[1024,128]{1,0:T(8,128)(2,1)S(1)}, u32[]{:S(2)}, u32[]{:S(2)}) collective-permute-start(bf16[1024,128]{1,0:T(8,128)(2,1)S(1)} %get-tuple-element.12), channel_id=1, source_target_pairs={{0,3},{1,2},{2,1},{3,0},{4,7},{5,6},{6,5},{7,4},{8,11},{9,10},{10,... | collective-permute-start | bytes 786440 | tf_op jit(solution)/shard_map/ppermute | solution.py:140
  21.7 0.0 copy-start.7
  22.4 0.0 copy-done.7
  22.4 0.1 reshape.28
  22.5 0.5 reshape.32.lim_ref
  23.0 0.1 pad_add_fusion.off_ref
  23.0 8.3 %collective-permute-done.2.side_ref = bf16[1024,128]{1,0:T(8,128)(2,1)S(1)} collective-permute-done((bf16[1024,128]{1,0:T(8,128)(2,1)S(1)}, bf16[1024,128]{1,0:T(8,128)(2,1)S(1)}, u32[]{:S(2)}, u32[]{:S(2)}) %collective-permute-start.2) | collective-permute-done | bytes 262176 | tf_op jit(solution)/shard_map/ppermute | solution.py:140
  31.3 0.0 all-to-all-done
  31.3 3.0 %near.1.near_ref = f32[1024,128]{1,0:T(8,128)S(1)} custom-call(s32[4]{0:T(128)S(1)} %pad_add_fusion.off_ref, bf16[1024,128]{1,0:T(8,128)(2,1)S(1)} %bitcast.13, bf16[1024,128]{1,0:T(8,128)(2,1)S(1)} %get-tuple-element.11.own_ref, bf16[1024,128]{1,0:T(8,128)(2,1)S(1)} %collective-permute-done.2.side_ref, s32[1024,1]{1,0:T(8,128)S(1)} %reshape.32.lim_ref), custom_call_target="tpu_custom_call" | custom-call | tf_op jit(solution)/shard_map/near/pallas_call | solution.py:149
  34.3 0.0 copy-start
  34.3 0.0 collective-permute-done.side_ref
  34.3 0.0 collective-permute-done.1.both_ref
  34.4 3.9 %far.1 = bf16[1024,128]{1,0:T(8,128)(2,1)} custom-call(s32[4]{0:T(128)S(1)} %pad_add_fusion.off_ref, bf16[1024,128]{1,0:T(8,128)(2,1)S(1)} %bitcast.14, bf16[1024,128]{1,0:T(8,128)(2,1)S(1)} %collective-permute-done.side_ref, bf16[1024,128]{1,0:T(8,128)(2,1)S(1)} %collective-permute-done.1.both_ref, s32[1024,1]{1,0:T(8,128)S(1)} %reshape.32.lim_ref, ...), custom_call_target="tpu_custom_call" | custom-call | tf_op jit(solution)/shard_map/far/pallas_call | solution.py:153
  38.2 0.0 copy-start.1
  38.2 0.0 copy-start.5
  38.2 7.4 %all-to-all-start.1 = ((bf16[16,64,128]{2,1,0:T(8,128)(2,1)}), bf16[16,64,128]{2,1,0:T(8,128)(2,1)S(1)}, u32[]{:S(2)}, u32[]{:S(2)}) async-start(bf16[16,64,128]{2,1,0:T(8,128)(2,1)} %bitcast.10), calls=%async_computation.1 | async-start | bytes 524288 | tf_op jit(solution)/shard_map/all_to_all | solution.py:119
  45.7 0.0 copy-done
  45.7 0.0 copy-done.1
  45.7 0.0 copy-done.5
  45.7 0.0 copy-start.4
  45.7 0.4 gate.1.gate_ref
  46.1 9.3 %all-to-all-done.1 = bf16[16,64,128]{2,1,0:T(8,128)(2,1)S(1)} async-done(((bf16[16,64,128]{2,1,0:T(8,128)(2,1)}), bf16[16,64,128]{2,1,0:T(8,128)(2,1)S(1)}, u32[]{:S(2)}, u32[]{:S(2)}) %all-to-all-start.1) | async-done | bytes 262176 | tf_op jit(solution)/shard_map/all_to_all | solution.py:119
  55.4 0.0 copy-done.4
  55.4 1.0 %finish.1 = bf16[64,512]{1,0:T(8,128)(2,1)} custom-call(bf16[4,4,64,128]{3,2,1,0:T(8,128)(2,1)S(1)} %bitcast.15, f32[64,512]{1,0:T(8,128)S(1)} %gate.1.gate_ref, bf16[64,512]{1,0:T(8,128)(2,1)S(1)} %copy-done.1, bf16[512,512]{1,0:T(8,128)(2,1)S(1)} %copy-done.4), custom_call_target="tpu_custom_call" | custom-call | tf_op jit(solution)/shard_map/finish/pallas_call | solution.py:158
  (2 shorter events, 0.0 us)
Async XLA Ops:
  0.0 11.3 %copy-start.3 = (bf16[512,512]{1,0:T(8,128)(2,1)S(1)}, bf16[512,512]{1,0:T(8,128)(2,1)}, u32[]{:S(2)}) copy-start(bf16[512,512]{1,0:T(8,128)(2,1)} %v_ref.1) | copy-start | bytes 1572868
  2.1 9.2 %copy-start.2 = (bf16[512,512]{1,0:T(8,128)(2,1)S(1)}, bf16[512,512]{1,0:T(8,128)(2,1)}, u32[]{:S(2)}) copy-start(bf16[512,512]{1,0:T(8,128)(2,1)} %k_ref.1) | copy-start | bytes 1572868
  2.1 29.2 %all-to-all-start = ((bf16[16,64,128]{2,1,0:T(8,128)(2,1)}), bf16[16,64,128]{2,1,0:T(8,128)(2,1)S(1)}, u32[]{:S(2)}, u32[]{:S(2)}) async-start(bf16[16,64,128]{2,1,0:T(8,128)(2,1)} %bitcast.5), calls=%async_computation | async-start | bytes 524288 | tf_op jit(solution)/shard_map/all_to_all | solution.py:119
  11.3 0.7 %copy-start.6 = (bf16[512]{0:T(512)(128)(2,1)S(1)}, bf16[512]{0:T(512)(128)(2,1)}, u32[]{:S(2)}) copy-start(bf16[512]{0:T(512)(128)(2,1)} %s_ref.1) | copy-start | bytes 3076
  12.4 21.9 %collective-permute-start = (bf16[1024,128]{1,0:T(8,128)(2,1)S(1)}, bf16[1024,128]{1,0:T(8,128)(2,1)S(1)}, u32[]{:S(2)}, u32[]{:S(2)}) collective-permute-start(bf16[1024,128]{1,0:T(8,128)(2,1)S(1)} %get-tuple-element.9), channel_id=1, source_target_pairs={{0,1},{1,0},{2,3},{3,2},{4,5},{5,4},{6,7},{7,6},{8,9},{9,8},{10,11... | collective-permute-start | bytes 786440 | tf_op jit(solution)/shard_map/ppermute | solution.py:139
  16.3 18.1 %collective-permute-start.1 = (bf16[1024,128]{1,0:T(8,128)(2,1)S(1)}, bf16[1024,128]{1,0:T(8,128)(2,1)S(1)}, u32[]{:S(2)}, u32[]{:S(2)}) collective-permute-start(bf16[1024,128]{1,0:T(8,128)(2,1)S(1)} %get-tuple-element.10), channel_id=1, source_target_pairs={{0,2},{2,0},{1,3},{3,1},{4,6},{6,4},{5,7},{7,5},{8,10},{10,8},{9,1... | collective-permute-start | bytes 786440 | tf_op jit(solution)/shard_map/ppermute | solution.py:141
  19.6 11.7 %collective-permute-start.2 = (bf16[1024,128]{1,0:T(8,128)(2,1)S(1)}, bf16[1024,128]{1,0:T(8,128)(2,1)S(1)}, u32[]{:S(2)}, u32[]{:S(2)}) collective-permute-start(bf16[1024,128]{1,0:T(8,128)(2,1)S(1)} %get-tuple-element.12), channel_id=1, source_target_pairs={{0,3},{1,2},{2,1},{3,0},{4,7},{5,6},{6,5},{7,4},{8,11},{9,10},{10,... | collective-permute-start | bytes 786440 | tf_op jit(solution)/shard_map/ppermute | solution.py:140
  21.7 0.7 %copy-start.7 = (s32[1024]{0:T(1024)S(1)}, s32[1024]{0:T(1024)}, u32[]{:S(2)}) copy-start(s32[1024]{0:T(1024)} %param.14) | copy-start | bytes 12292
  34.3 11.3 %copy-start = (bf16[512,1024]{1,0:T(8,128)(2,1)S(1)}, bf16[512,1024]{1,0:T(8,128)(2,1)}, u32[]{:S(2)}) copy-start(bf16[512,1024]{1,0:T(8,128)(2,1)} %w_ref.2) | copy-start | bytes 3145732
  38.2 7.5 %copy-start.1 = (bf16[64,512]{1,0:T(8,128)(2,1)S(1)}, bf16[64,512]{1,0:T(8,128)(2,1)}, u32[]{:S(2)}) copy-start(bf16[64,512]{1,0:T(8,128)(2,1)} %x_ref.3) | copy-start | bytes 196612
  38.2 7.5 %copy-start.5 = (f32[512]{0:T(512)S(1)}, f32[512]{0:T(512)}, u32[]{:S(2)}) copy-start(f32[512]{0:T(512)} %param.15) | copy-start | bytes 6148
  38.2 17.1 %all-to-all-start.1 = ((bf16[16,64,128]{2,1,0:T(8,128)(2,1)}), bf16[16,64,128]{2,1,0:T(8,128)(2,1)S(1)}, u32[]{:S(2)}, u32[]{:S(2)}) async-start(bf16[16,64,128]{2,1,0:T(8,128)(2,1)} %bitcast.10), calls=%async_computation.1 | async-start | bytes 524288 | tf_op jit(solution)/shard_map/all_to_all | solution.py:119
  45.7 9.7 %copy-start.4 = (bf16[512,512]{1,0:T(8,128)(2,1)S(1)}, bf16[512,512]{1,0:T(8,128)(2,1)}, u32[]{:S(2)}) copy-start(bf16[512,512]{1,0:T(8,128)(2,1)} %w_ref.3) | copy-start | bytes 1572868

commit v4 on v3

--- a/solution.py
+++ b/solution.py
@@ -20,13 +20,14 @@
     return (v - mean) / jnp.sqrt(var + 1e-5)
 
 
-def project_kernel(x_hbm, gain_hbm, w_hbm, q_ref, x_ref, gain_ref, w_ref, sems):
+def front_kernel(
+    part_ref, x_hbm, gain_hbm, w_hbm, k_hbm, v_hbm, s_hbm, q_hbm, own_ref, side_ref, z_ref, both_ref,
+    x_ref, gain_ref, w_ref, k_ref, v_ref, s_ref, q_ref, sems, q_sems,
+):
     width = w_ref.shape[1]
-    loads = [
-        pltpu.make_async_copy(x_hbm, x_ref, sems.at[0]),
-        pltpu.make_async_copy(gain_hbm, gain_ref, sems.at[1]),
-        pltpu.make_async_copy(w_hbm.at[:, pl.ds(0, width)], w_ref, sems.at[2]),
-    ]
+    sources = (x_hbm, gain_hbm, w_hbm.at[:, pl.ds(0, width)], k_hbm, s_hbm, v_hbm)
+    targets = (x_ref, gain_ref, w_ref, k_ref, s_ref, v_ref)
+    loads = [pltpu.make_async_copy(a, b, sems.at[i]) for i, (a, b) in enumerate(zip(sources, targets))]
     for load in loads:
         load.start()
     loads[0].wait()
@@ -35,10 +36,17 @@
     loads[2].wait()
     p = jnp.dot(normed, w_ref[...], preferred_element_type=F32)
     q = (p / (1.0 + jnp.exp(-p))).astype(BF16)
-    parts, copies, _, part = q_ref.shape
+    parts, _, part = q_ref.shape
     for h in range(parts):
-        for i in range(copies):
-            q_ref[h, i] = q[:, h * part:(h + 1) * part]
+        q_ref[h] = q[:, h * part:(h + 1) * part]
+    stores = [pltpu.make_async_copy(q_ref, q_hbm.at[:, i], q_sems.at[i]) for i in range(q_hbm.shape[1])]
+    for store in stores:
+        store.start()
+    for load in loads[3:]:
+        load.wait()
+    pack(part_ref, k_ref, v_ref, s_ref, own_ref, side_ref, z_ref, both_ref)
+    for store in stores:
+        store.wait()
 
 
 def gate_kernel(x_ref, gain_ref, w_ref, gate_ref):
@@ -48,7 +56,7 @@
     gate_ref[...] = p / (1.0 + jnp.exp(-p))
 
 
-def pack_kernel(part_ref, k_ref, v_ref, s_ref, *outs):
+def pack(part_ref, k_ref, v_ref, s_ref, *outs):
     rows, width = k_ref.shape
     part = width // len(outs)
     col = jnp.broadcast_to(s_ref[...].astype(F32).reshape(1, rows) * (1.0 / 16.0), (8, rows)).T[:, :1]
@@ -119,23 +127,23 @@
         return lax.all_to_all(t.reshape(4 * pairs, own, part), ("z", "side", "pair"), 0, 0, tiled=True)
 
     gain = ln_gain.reshape(1, width)
-    q = pl.pallas_call(
-        project_kernel, out_shape=sds((4, pairs, own, part)), in_specs=[HB] * 3, out_specs=VM,
+    hbm = [pltpu.with_memory_space_constraint(v, pltpu.HBM) for v in (cand_x, gain, w_qu, hist_keys, hist_values, key_scale)]
+    q, own_kv, to_side, to_z, to_both = pl.pallas_call(
+        front_kernel, out_shape=(sds((4, pairs, own, part)),) + (sds((2 * n, part)),) * 4,
+        in_specs=[SM] + [HB] * 6, out_specs=(HB,) + (VM,) * 4,
         scratch_shapes=[
             pltpu.VMEM((own, width), BF16), pltpu.VMEM((1, width), F32), pltpu.VMEM((width, width), BF16),
-            pltpu.SemaphoreType.DMA((3,)),
+            pltpu.VMEM((n, width), BF16), pltpu.VMEM((n, width), BF16), pltpu.VMEM((n,), BF16),
+            pltpu.VMEM((4, own, part), BF16),
+            pltpu.SemaphoreType.DMA((6,)), pltpu.SemaphoreType.DMA((pairs,)),
         ],
-        compiler_params=PARAMS, name="project",
-    )(*(pltpu.with_memory_space_constraint(v, pltpu.HBM) for v in (cand_x, gain, w_qu)))
+        compiler_params=PARAMS, name="front",
+    )((z * 2 + side).astype(jnp.int32).reshape(1), *hbm)
     gate = pl.pallas_call(
         gate_kernel, out_shape=sds((own, width), F32), in_specs=[VM] * 3, out_specs=VM,
         compiler_params=PARAMS, name="gate",
     )(cand_x, gain, w_qu)
     every_q = exchange(q).reshape(rows, part)
-    own_kv, to_side, to_z, to_both = pl.pallas_call(
-        pack_kernel, out_shape=(sds((2 * n, part)),) * 4,
-        in_specs=[SM] + [VM] * 3, out_specs=(VM,) * 4, compiler_params=PARAMS, name="pack",
-    )((z * 2 + side).astype(jnp.int32).reshape(1), hist_keys, hist_values, key_scale)
     z_kv = lax.ppermute(to_z, "z", [(0, 1), (1, 0)])
     both_kv = lax.ppermute(to_both, ("side", "z"), [(i, 3 - i) for i in range(4)])
     side_kv = lax.ppermute(to_side, "side", [(0, 1), (1, 0)])

time: 56.9 us -> 56.1 us (0.986)
  waiting for transfers between devices: 17.5 us -> 19.2 us
  starting transfers between devices: 25.8 us -> 24.6 us
  local copies, waits for them, and re-layouts: 1.27 us -> 0.6 us
    all_to_all x2, starting transfers between devices: 16.6 us -> 15.4 us  [exchange(): lax.all_to_all(t.reshape(4 * pairs, own, part), ('z', 'side', 'pair'), 0,...]
    ppermute x1, waiting for transfers between devices: 8.29 us -> 9.41 us  [layer(): lax.ppermute(to_both, ('side', 'z'), [(i, 3 - i) for i in range(4)])]
    unnamed x16 -> x10, local copies, waits for them, and re-layouts: 0.71 us -> 0.04 us
    pallas_call x2 -> x1, Pallas kernels: 2.55 us -> 2.13 us  [layer(): pl.pallas_call(front_kernel, out_shape=(sds((4, pairs, own, part)),) + (s...]
  transfers between devices with their start and end apart: 5 -> 5, of which waited for: 2 -> 2; matrix products, arithmetic and copies ran while one was open for 1% -> 1% of each run, Pallas kernels for 7% -> 6%
where the time goes in v4:
time: 56.1 us; the launch traced here: 55.6 us
  starting transfers between devices  24.6 us (44%)
  waiting for transfers between devices  19.2 us (34%)
  Pallas kernels  10.4 us (19%)
  between operations  0.82 us (1%)
  local copies, waits for them, and re-layouts  0.6 us (1%)
    all_to_all x2, starting transfers between devices, exchange(): lax.all_to_all(t.reshape(4 * pairs, own, part), ('z', 'side', 'pair'), 0,...  15.4 us
    all_to_all x2, waiting for transfers between devices, exchange(): lax.all_to_all(t.reshape(4 * pairs, own, part), ('z', 'side', 'pair'), 0,...  9.78 us
    ppermute x1, waiting for transfers between devices, layer(): lax.ppermute(to_both, ('side', 'z'), [(i, 3 - i) for i in range(4)])  9.41 us
    pallas_call x1, Pallas kernels, layer(): pl.pallas_call(far_kernel, out_shape=sds((rows, part)), in_specs=[SM] + [...  3.85 us
    ppermute x1, starting transfers between devices, layer(): z_kv = lax.ppermute(to_z, 'z', [(0, 1), (1, 0)])  3.83 us
    ppermute x1, starting transfers between devices, layer(): side_kv = lax.ppermute(to_side, 'side', [(0, 1), (1, 0)])  3.37 us
    pallas_call x1, Pallas kernels, layer(): pl.pallas_call(near_kernel, out_shape=sds((rows, part), F32), in_specs=[S...  2.99 us
    pallas_call x1, Pallas kernels, layer(): pl.pallas_call(front_kernel, out_shape=(sds((4, pairs, own, part)),) + (s...  2.13 us
  transfers between devices with their start and end apart: 5, of which 2 were waited for; matrix products, arithmetic and copies ran while one was open for 1% of the time, Pallas kernels for 6%

profile of v4, /device:TPU:6, one launch (start us, length us, event | category | flops | bytes accessed | tf_op | source)
XLA Modules:
  0.0 55.6 jit_solution(12943726752142252692)
XLA Ops:
  0.0 2.1 %front.1 = (bf16[4,4,64,128]{3,2,1,0:T(8,128)(2,1)}, bf16[1024,128]{1,0:T(8,128)(2,1)S(1)}, bf16[1024,128]{1,0:T(8,128)(2,1)S(1)}, bf16[1024,128]{1,0:T(8,128)(2,1)S(1)}, bf16[1024,128]{1,0:T(8,128)(2,1)S(1)}) custom-call(s32[1]{0:T(128)} %bitcast.4.part_ref, bf16[64,512]{1,0:T(8,128)(2,1)} %x_ref.3, f32[1,512]{1,0:T(1,128)} %bitcast.16, ...), custom_call_target="tpu_custom_call" | custom-call | tf_op jit(solution)/shard_map/front/pallas_call | solution.py:131
  2.1 9.0 %all-to-all-start = ((bf16[16,64,128]{2,1,0:T(8,128)(2,1)}), bf16[16,64,128]{2,1,0:T(8,128)(2,1)S(1)}, u32[]{:S(2)}, u32[]{:S(2)}) async-start(bf16[16,64,128]{2,1,0:T(8,128)(2,1)} %bitcast.6), calls=%async_computation | async-start | bytes 524288 | tf_op jit(solution)/shard_map/all_to_all | solution.py:127
  11.2 3.8 %collective-permute-start = (bf16[1024,128]{1,0:T(8,128)(2,1)S(1)}, bf16[1024,128]{1,0:T(8,128)(2,1)S(1)}, u32[]{:S(2)}, u32[]{:S(2)}) collective-permute-start(bf16[1024,128]{1,0:T(8,128)(2,1)S(1)} %get-tuple-element.11), channel_id=1, source_target_pairs={{0,1},{1,0},{2,3},{3,2},{4,5},{5,4},{6,7},{7,6},{8,9},{9,8},{10,11... | collective-permute-start | bytes 786440 | tf_op jit(solution)/shard_map/ppermute | solution.py:147
  15.0 3.4 %collective-permute-start.1 = (bf16[1024,128]{1,0:T(8,128)(2,1)S(1)}, bf16[1024,128]{1,0:T(8,128)(2,1)S(1)}, u32[]{:S(2)}, u32[]{:S(2)}) collective-permute-start(bf16[1024,128]{1,0:T(8,128)(2,1)S(1)} %get-tuple-element.12), channel_id=1, source_target_pairs={{0,2},{2,0},{1,3},{3,1},{4,6},{6,4},{5,7},{7,5},{8,10},{10,8},{9,1... | collective-permute-start | bytes 786440 | tf_op jit(solution)/shard_map/ppermute | solution.py:149
  18.4 2.0 %collective-permute-start.2 = (bf16[1024,128]{1,0:T(8,128)(2,1)S(1)}, bf16[1024,128]{1,0:T(8,128)(2,1)S(1)}, u32[]{:S(2)}, u32[]{:S(2)}) collective-permute-start(bf16[1024,128]{1,0:T(8,128)(2,1)S(1)} %get-tuple-element.14), channel_id=1, source_target_pairs={{0,3},{1,2},{2,1},{3,0},{4,7},{5,6},{6,5},{7,4},{8,11},{9,10},{10,... | collective-permute-start | bytes 786440 | tf_op jit(solution)/shard_map/ppermute | solution.py:148
  20.4 0.0 copy-start.4
  21.1 0.0 copy-done.4
  21.1 0.1 reshape.28
  21.2 0.5 reshape.32.lim_ref
  21.7 0.1 pad_add_fusion.off_ref
  21.8 9.4 %collective-permute-done.2.side_ref = bf16[1024,128]{1,0:T(8,128)(2,1)S(1)} collective-permute-done((bf16[1024,128]{1,0:T(8,128)(2,1)S(1)}, bf16[1024,128]{1,0:T(8,128)(2,1)S(1)}, u32[]{:S(2)}, u32[]{:S(2)}) %collective-permute-start.2) | collective-permute-done | bytes 262176 | tf_op jit(solution)/shard_map/ppermute | solution.py:148
  31.2 0.0 all-to-all-done
  31.2 3.0 %near.1.near_ref = f32[1024,128]{1,0:T(8,128)S(1)} custom-call(s32[4]{0:T(128)S(1)} %pad_add_fusion.off_ref, bf16[1024,128]{1,0:T(8,128)(2,1)S(1)} %bitcast.13, bf16[1024,128]{1,0:T(8,128)(2,1)S(1)} %get-tuple-element.13.own_ref, bf16[1024,128]{1,0:T(8,128)(2,1)S(1)} %collective-permute-done.2.side_ref, s32[1024,1]{1,0:T(8,128)S(1)} %reshape.32.lim_ref), custom_call_target="tpu_custom_call" | custom-call | tf_op jit(solution)/shard_map/near/pallas_call | solution.py:157
  34.2 0.0 copy-start
  34.2 0.0 collective-permute-done.side_ref
  34.2 0.0 collective-permute-done.1.both_ref
  34.2 3.9 %far.1 = bf16[1024,128]{1,0:T(8,128)(2,1)} custom-call(s32[4]{0:T(128)S(1)} %pad_add_fusion.off_ref, bf16[1024,128]{1,0:T(8,128)(2,1)S(1)} %bitcast.14, bf16[1024,128]{1,0:T(8,128)(2,1)S(1)} %collective-permute-done.side_ref, bf16[1024,128]{1,0:T(8,128)(2,1)S(1)} %collective-permute-done.1.both_ref, s32[1024,1]{1,0:T(8,128)S(1)} %reshape.32.lim_ref, ...), custom_call_target="tpu_custom_call" | custom-call | tf_op jit(solution)/shard_map/far/pallas_call | solution.py:161
  38.1 0.0 copy-start.1
  38.1 0.0 copy-start.3
  38.1 6.3 %all-to-all-start.1 = ((bf16[16,64,128]{2,1,0:T(8,128)(2,1)}), bf16[16,64,128]{2,1,0:T(8,128)(2,1)S(1)}, u32[]{:S(2)}, u32[]{:S(2)}) async-start(bf16[16,64,128]{2,1,0:T(8,128)(2,1)} %bitcast.10), calls=%async_computation.1 | async-start | bytes 524288 | tf_op jit(solution)/shard_map/all_to_all | solution.py:127
  44.4 0.0 copy-done
  44.4 0.0 copy-done.1
  44.4 0.0 copy-done.3
  44.4 0.0 copy-start.2
  44.4 0.4 gate.1.gate_ref
  44.8 9.8 %all-to-all-done.1 = bf16[16,64,128]{2,1,0:T(8,128)(2,1)S(1)} async-done(((bf16[16,64,128]{2,1,0:T(8,128)(2,1)}), bf16[16,64,128]{2,1,0:T(8,128)(2,1)S(1)}, u32[]{:S(2)}, u32[]{:S(2)}) %all-to-all-start.1) | async-done | bytes 262176 | tf_op jit(solution)/shard_map/all_to_all | solution.py:127
  54.6 0.0 copy-done.2
  54.6 1.0 %finish.1 = bf16[64,512]{1,0:T(8,128)(2,1)} custom-call(bf16[4,4,64,128]{3,2,1,0:T(8,128)(2,1)S(1)} %bitcast.15, f32[64,512]{1,0:T(8,128)S(1)} %gate.1.gate_ref, bf16[64,512]{1,0:T(8,128)(2,1)S(1)} %copy-done.1, bf16[512,512]{1,0:T(8,128)(2,1)S(1)} %copy-done.2), custom_call_target="tpu_custom_call" | custom-call | tf_op jit(solution)/shard_map/finish/pallas_call | solution.py:166
  (2 shorter events, 0.0 us)
Async XLA Ops:
  2.1 29.0 %all-to-all-start = ((bf16[16,64,128]{2,1,0:T(8,128)(2,1)}), bf16[16,64,128]{2,1,0:T(8,128)(2,1)S(1)}, u32[]{:S(2)}, u32[]{:S(2)}) async-start(bf16[16,64,128]{2,1,0:T(8,128)(2,1)} %bitcast.6), calls=%async_computation | async-start | bytes 524288 | tf_op jit(solution)/shard_map/all_to_all | solution.py:127
  11.2 23.0 %collective-permute-start = (bf16[1024,128]{1,0:T(8,128)(2,1)S(1)}, bf16[1024,128]{1,0:T(8,128)(2,1)S(1)}, u32[]{:S(2)}, u32[]{:S(2)}) collective-permute-start(bf16[1024,128]{1,0:T(8,128)(2,1)S(1)} %get-tuple-element.11), channel_id=1, source_target_pairs={{0,1},{1,0},{2,3},{3,2},{4,5},{5,4},{6,7},{7,6},{8,9},{9,8},{10,11... | collective-permute-start | bytes 786440 | tf_op jit(solution)/shard_map/ppermute | solution.py:147
  15.0 19.2 %collective-permute-start.1 = (bf16[1024,128]{1,0:T(8,128)(2,1)S(1)}, bf16[1024,128]{1,0:T(8,128)(2,1)S(1)}, u32[]{:S(2)}, u32[]{:S(2)}) collective-permute-start(bf16[1024,128]{1,0:T(8,128)(2,1)S(1)} %get-tuple-element.12), channel_id=1, source_target_pairs={{0,2},{2,0},{1,3},{3,1},{4,6},{6,4},{5,7},{7,5},{8,10},{10,8},{9,1... | collective-permute-start | bytes 786440 | tf_op jit(solution)/shard_map/ppermute | solution.py:149
  18.4 12.8 %collective-permute-start.2 = (bf16[1024,128]{1,0:T(8,128)(2,1)S(1)}, bf16[1024,128]{1,0:T(8,128)(2,1)S(1)}, u32[]{:S(2)}, u32[]{:S(2)}) collective-permute-start(bf16[1024,128]{1,0:T(8,128)(2,1)S(1)} %get-tuple-element.14), channel_id=1, source_target_pairs={{0,3},{1,2},{2,1},{3,0},{4,7},{5,6},{6,5},{7,4},{8,11},{9,10},{10,... | collective-permute-start | bytes 786440 | tf_op jit(solution)/shard_map/ppermute | solution.py:148
  20.4 0.7 %copy-start.4 = (s32[1024]{0:T(1024)S(1)}, s32[1024]{0:T(1024)}, u32[]{:S(2)}) copy-start(s32[1024]{0:T(1024)} %param.14) | copy-start | bytes 12292
  34.2 10.2 %copy-start = (bf16[512,1024]{1,0:T(8,128)(2,1)S(1)}, bf16[512,1024]{1,0:T(8,128)(2,1)}, u32[]{:S(2)}) copy-start(bf16[512,1024]{1,0:T(8,128)(2,1)} %w_ref.2) | copy-start | bytes 3145732
  38.1 6.4 %copy-start.1 = (bf16[64,512]{1,0:T(8,128)(2,1)S(1)}, bf16[64,512]{1,0:T(8,128)(2,1)}, u32[]{:S(2)}) copy-start(bf16[64,512]{1,0:T(8,128)(2,1)} %x_ref.3) | copy-start | bytes 196612
  38.1 6.4 %copy-start.3 = (f32[512]{0:T(512)S(1)}, f32[512]{0:T(512)}, u32[]{:S(2)}) copy-start(f32[512]{0:T(512)} %param.15) | copy-start | bytes 6148
  38.1 16.5 %all-to-all-start.1 = ((bf16[16,64,128]{2,1,0:T(8,128)(2,1)}), bf16[16,64,128]{2,1,0:T(8,128)(2,1)S(1)}, u32[]{:S(2)}, u32[]{:S(2)}) async-start(bf16[16,64,128]{2,1,0:T(8,128)(2,1)} %bitcast.10), calls=%async_computation.1 | async-start | bytes 524288 | tf_op jit(solution)/shard_map/all_to_all | solution.py:127
  44.4 10.2 %copy-start.2 = (bf16[512,512]{1,0:T(8,128)(2,1)S(1)}, bf16[512,512]{1,0:T(8,128)(2,1)}, u32[]{:S(2)}) copy-start(bf16[512,512]{1,0:T(8,128)(2,1)} %w_ref.3) | copy-start | bytes 1572868
